TPU v7x, 32 devices: a 4x4x1 block of a 4x4x8 slice. The times are simulated.
32 devices in a mesh: pair: 1 (over z), tp: 4 (over y), side: 8 (over x, core).
Axes of the slice: x: 4, y: 4, z: 1, core: 2. Of those that a mesh axis runs over, the one named last changes fastest.
The devices are a block of a 4x4x8 slice.
Arguments:
- x_prompt: bfloat16 [4096, 4096], P(('pair', 'side'))
- s_len: int32 [8], P(('pair', 'side'))
- y_tok: bfloat16 [64, 4096], P(('pair', 'side'))
- k_cache: bfloat16 [1, 64, 768, 2, 4, 128], P(None, ('pair', 'side'), None, None, 'tp')
- v_cache: bfloat16 [1, 64, 768, 2, 4, 128], P(None, ('pair', 'side'), None, None, 'tp')
- c_len: int32 [64], P(('pair', 'side'))
- wqkv_a: bfloat16 [1, 4096, 8, 768], P(None, None, 'tp')
- wo_a: bfloat16 [1, 8, 512, 4096], P(None, 'tp')
- wug_a: bfloat16 [1, 4096, 2, 14336], P(None, None, None, 'tp')
- wd_a: bfloat16 [1, 14336, 4096], P(None, 'tp')
- norm_a: bfloat16 [1, 2, 4096], replicated
- wqkv_b: bfloat16 [1, 4096, 2, 4, 768], P(None, None, None, 'tp')
- wo_b: bfloat16 [1, 2, 4, 512, 4096], P(None, None, 'tp')
- wug_b: bfloat16 [1, 4096, 2, 14336], P(None, None, None, 'tp')
- wd_b: bfloat16 [1, 14336, 4096], P(None, 'tp')
- norm_b: bfloat16 [1, 2, 4096], replicated
Outputs:
- output 1: bfloat16 [4096, 4096], P(('pair', 'side'))
- output 2: bfloat16 [64, 4096], P(('pair', 'side'))
- output 3: bfloat16 [1, 4096, 2, 4, 128], P(None, ('pair', 'side'), None, 'tp')
- output 4: bfloat16 [1, 4096, 2, 4, 128], P(None, ('pair', 'side'), None, 'tp')
- output 5: bfloat16 [1, 64, 768, 2, 4, 128], P(None, ('pair', 'side'), None, None, 'tp')
- output 6: bfloat16 [1, 64, 768, 2, 4, 128], P(None, ('pair', 'side'), None, None, 'tp')
All inputs are finite; a program needn't handle non-finite values.
Results may differ from a plain program's by a relative error of at most 0.0075918.
Values are sent between devices in bfloat16 or wider.
A program may use at most 768 MiB of HBM per device.

v0:
```python
import jax
import jax.numpy as jnp
from jax import lax
from jax.sharding import PartitionSpec as P

ROPE_BASE = 10000.0
NORM_EPS = 1e-5


def rms_norm(hidden, gain):
    val_f32 = hidden.astype(jnp.float32)
    inv_rms = lax.rsqrt(jnp.mean(val_f32 * val_f32, axis=-1, keepdims=True) + NORM_EPS)
    return (val_f32 * inv_rms * gain.astype(jnp.float32)).astype(jnp.bfloat16)


def rope_rot(vals_in, positions):
    half_dim = vals_in.shape[-1] // 2
    inv_freq = ROPE_BASE ** (-jnp.arange(half_dim, dtype=jnp.float32) / half_dim)
    angles = positions.astype(jnp.float32)[:, None] * inv_freq[None, :]
    tab_shape = (angles.shape[0],) + (1,) * (vals_in.ndim - 2) + (half_dim,)
    cos_tab = jnp.cos(angles).reshape(tab_shape)
    sin_tab = jnp.sin(angles).reshape(tab_shape)
    lo_half = vals_in[..., :half_dim].astype(jnp.float32)
    hi_half = vals_in[..., half_dim:].astype(jnp.float32)
    return jnp.concatenate([lo_half * cos_tab - hi_half * sin_tab, hi_half * cos_tab + lo_half * sin_tab], axis=-1).astype(jnp.bfloat16)


def mlp_block(hidden, w_ug, w_down, gain, combine):
    normed = rms_norm(hidden, gain)
    upgate = jnp.einsum('sd,dkf->skf', normed, w_ug, preferred_element_type=jnp.float32).astype(jnp.bfloat16)
    act_out = (jax.nn.silu(upgate[:, 1].astype(jnp.float32)) * upgate[:, 0].astype(jnp.float32)).astype(jnp.bfloat16)
    mlp_down = combine(jnp.dot(act_out, w_down, preferred_element_type=jnp.float32)).astype(jnp.bfloat16)
    return (hidden.astype(jnp.float32) + mlp_down.astype(jnp.float32)).astype(jnp.bfloat16)


def prompt_layer(hidden, q_start, prev_k, prev_v, seq_len, w_qkv, w_out, w_ug, w_down, gain_pair, combine):
    num_rows = hidden.shape[0]
    kv_loc = w_qkv.shape[1]
    head_dim = (w_qkv.shape[2] - w_out.shape[1]) // 2
    group = w_out.shape[1] // head_dim
    positions = q_start + jnp.arange(num_rows)
    normed = rms_norm(hidden, gain_pair[0])
    qkv_all = jnp.einsum('sd,dhe->she', normed, w_qkv, preferred_element_type=jnp.float32).astype(jnp.bfloat16)
    qkv_all = qkv_all.reshape(num_rows, kv_loc, group + 2, head_dim)
    queries = rope_rot(qkv_all[:, :, :group], positions)
    key_new = rope_rot(qkv_all[:, :, group], positions)
    val_new = qkv_all[:, :, group + 1]
    if prev_k is None:
        key_all = key_new
        val_all = val_new
    else:
        key_all = jnp.concatenate([prev_k, key_new], axis=0)
        val_all = jnp.concatenate([prev_v, val_new], axis=0)
    key_pos = jnp.arange(key_all.shape[0])
    allowed = (key_pos[None, :] <= positions[:, None]) & (key_pos[None, :] < seq_len)
    scores = jnp.einsum('qhgd,khd->hgqk', queries, key_all, preferred_element_type=jnp.float32) * head_dim ** -0.5
    scores = jnp.where(allowed, scores, -1e30)
    attn_prob = jax.nn.softmax(scores, axis=-1).astype(jnp.bfloat16)
    attn_out = jnp.einsum('hgqk,khd->qhgd', attn_prob, val_all, preferred_element_type=jnp.float32).astype(jnp.bfloat16)
    attn_proj = combine(jnp.einsum('qhf,hfd->qd', attn_out.reshape(num_rows, kv_loc, group * head_dim), w_out, preferred_element_type=jnp.float32)).astype(jnp.bfloat16)
    hidden = (hidden.astype(jnp.float32) + attn_proj.astype(jnp.float32)).astype(jnp.bfloat16)
    hidden = mlp_block(hidden, w_ug, w_down, gain_pair[1], combine)
    return hidden, key_new, val_new


def prefill_side(x_rows, seq_len, wqkv, wo, wug, wd, norms, combine):
    num_layers = wqkv.shape[0]
    half_len = x_rows.shape[0] // 2
    hidden_first = x_rows[:half_len]
    first_keys = []
    first_vals = []
    for layer_idx in range(num_layers):
        hidden_first, key_new, val_new = prompt_layer(hidden_first, 0, None, None, seq_len, wqkv[layer_idx], wo[layer_idx], wug[layer_idx], wd[layer_idx], norms[layer_idx], combine)
        first_keys.append(key_new)
        first_vals.append(val_new)
    hidden_second = x_rows[half_len:]
    key_layers = []
    val_layers = []
    for layer_idx in range(num_layers):
        hidden_second, key_new, val_new = prompt_layer(hidden_second, half_len, first_keys[layer_idx], first_vals[layer_idx], seq_len, wqkv[layer_idx], wo[layer_idx], wug[layer_idx], wd[layer_idx], norms[layer_idx], combine)
        key_layers.append(jnp.concatenate([first_keys[layer_idx], key_new], axis=0))
        val_layers.append(jnp.concatenate([first_vals[layer_idx], val_new], axis=0))
    valid = (jnp.arange(x_rows.shape[0]) < seq_len)[None, :, None, None]
    zero_val = jnp.zeros((), jnp.bfloat16)
    key_cache = jnp.where(valid, jnp.stack(key_layers), zero_val)
    val_cache = jnp.where(valid, jnp.stack(val_layers), zero_val)
    return jnp.concatenate([hidden_first, hidden_second], axis=0), key_cache, val_cache


def decode_side(tokens, lengths, k_cache, v_cache, wqkv, wo, wug, wd, norms, combine):
    num_layers = wqkv.shape[0]
    batch_rows = tokens.shape[0]
    kv_loc = wqkv.shape[2]
    tp_loc = wqkv.shape[3]
    head_dim = (wqkv.shape[4] - wo.shape[3]) // 2
    group = wo.shape[3] // head_dim
    slot_pos = jnp.arange(k_cache.shape[2])
    write_slot = (slot_pos[None, :] == lengths[:, None])[:, :, None, None, None]
    visible = (slot_pos[None, :] <= lengths[:, None])[:, None, None, None, :]
    hidden = tokens
    new_keys = []
    new_vals = []
    for layer_idx in range(num_layers):
        normed = rms_norm(hidden, norms[layer_idx, 0])
        qkv_all = jnp.einsum('bd,dije->bije', normed, wqkv[layer_idx], preferred_element_type=jnp.float32).astype(jnp.bfloat16)
        qkv_all = qkv_all.reshape(batch_rows, kv_loc, tp_loc, group + 2, head_dim)
        queries = rope_rot(qkv_all[:, :, :, :group], lengths)
        key_new = rope_rot(qkv_all[:, :, :, group], lengths)
        val_new = qkv_all[:, :, :, group + 1]
        key_upd = jnp.where(write_slot, key_new[:, None], k_cache[layer_idx])
        val_upd = jnp.where(write_slot, val_new[:, None], v_cache[layer_idx])
        scores = jnp.einsum('bijge,bsije->bijgs', queries, key_upd, preferred_element_type=jnp.float32) * head_dim ** -0.5
        scores = jnp.where(visible, scores, -1e30)
        attn_prob = jax.nn.softmax(scores, axis=-1).astype(jnp.bfloat16)
        attn_out = jnp.einsum('bijgs,bsije->bijge', attn_prob, val_upd, preferred_element_type=jnp.float32).astype(jnp.bfloat16)
        attn_proj = combine(jnp.einsum('bijf,ijfd->bd', attn_out.reshape(batch_rows, kv_loc, tp_loc, group * head_dim), wo[layer_idx], preferred_element_type=jnp.float32)).astype(jnp.bfloat16)
        hidden = (hidden.astype(jnp.float32) + attn_proj.astype(jnp.float32)).astype(jnp.bfloat16)
        hidden = mlp_block(hidden, wug[layer_idx], wd[layer_idx], norms[layer_idx, 1], combine)
        new_keys.append(key_upd)
        new_vals.append(val_upd)
    return hidden, jnp.stack(new_keys), jnp.stack(new_vals)


def tp_relayout(block, tp_size):
    num_layers, seq_rows, kv_loc, head_dim = block.shape
    if kv_loc % tp_size == 0:
        split_view = block.reshape(num_layers, seq_rows, kv_loc // tp_size, tp_size, head_dim)
        return lax.all_to_all(split_view, 'tp', 3, 2, tiled=True)
    ratio = tp_size // kv_loc
    tp_idx = lax.axis_index('tp')
    src_block = tp_idx // ratio
    dst_pos = tp_idx % kv_loc
    gathered = jnp.zeros_like(block)
    for round_idx in range(kv_loc):
        piece = lax.dynamic_slice_in_dim(block, (round_idx + src_block) % kv_loc, 1, axis=2)
        perm_pairs = [(src, (src % ratio) * kv_loc + (round_idx + src // ratio) % kv_loc) for src in range(tp_size)]
        received = lax.ppermute(piece, 'tp', perm_pairs)
        gathered = lax.dynamic_update_slice_in_dim(gathered, received, (dst_pos - round_idx) % kv_loc, axis=2)
    return gathered[:, :, :, None]


def hand_off(block, tp_size, side_size):
    shift_pairs = [(src, (src + side_size // 2) % side_size) for src in range(side_size)]
    moved = lax.ppermute(block, 'side', shift_pairs)
    return tp_relayout(moved, tp_size)


def solution(mesh):
    tp_size = mesh.shape['tp']
    side_size = mesh.shape['side']
    rows_spec = P(('pair', 'side'), None)
    flat_spec = P(('pair', 'side'))
    cache_spec = P(None, ('pair', 'side'), None, None, 'tp', None)
    prompt_spec = P(None, ('pair', 'side'), None, 'tp', None)
    in_specs = (rows_spec, flat_spec, rows_spec, cache_spec, cache_spec, flat_spec,
                P(None, None, 'tp', None), P(None, 'tp', None, None), P(None, None, None, 'tp'), P(None, 'tp', None), P(),
                P(None, None, None, 'tp', None), P(None, None, 'tp', None, None), P(None, None, None, 'tp'), P(None, 'tp', None), P())
    out_specs = (rows_spec, rows_spec, prompt_spec, prompt_spec, cache_spec, cache_spec)

    def tp_sum(part_sum):
        return lax.psum(part_sum, 'tp')

    def body(x_prompt, s_len, y_tok, k_cache, v_cache, c_len, wqkv_a, wo_a, wug_a, wd_a, norm_a, wqkv_b, wo_b, wug_b, wd_b, norm_b):
        hidden, key_cache, val_cache = prefill_side(x_prompt, s_len[0], wqkv_a, wo_a, wug_a, wd_a, norm_a, tp_sum)
        k_prompt = hand_off(key_cache, tp_size, side_size)
        v_prompt = hand_off(val_cache, tp_size, side_size)
        y_out, k_new, v_new = decode_side(y_tok, c_len, k_cache, v_cache, wqkv_b, wo_b, wug_b, wd_b, norm_b, tp_sum)
        return hidden, y_out, k_prompt, v_prompt, k_new, v_new

    return jax.shard_map(body, mesh=mesh, in_specs=in_specs, out_specs=out_specs, check_vma=False)
```

profile of v0, /device:TPU:100, one launch (start us, length us, event | category | flops | bytes accessed | tf_op | source)
XLA Modules:
  0.0 612.5 jit_solution(10377724239460760996)
XLA Ops:
  0.7 3.3 fusion.45
  3.9 1.4 slice_convert_fusion.2
  5.4 8.1 %fusion.108 = bf16[256,2,768]{2,0,1:T(8,128)(2,1)S(1)} fusion(bf16[4096,2,768]{2,1,0:T(2,128)(2,1)} %bitcast.195, f32[256]{0:T(256)S(1)} %get-tuple-element.76, f32[4096]{0:T(1024)S(1)} %bitcast.191, bf16[512,4096]{1,0:T(8,128)(2,1)S(1)} %copy-done), kind=kOutput, calls=%fused_computation.113 | convolution fusion | flops 3225812992 | bytes 15483904 | tf_op jit(solution)/shard_map/sd,dhe->she/dot_general | solution.py:43
  13.4 0.3 copy.63
  13.7 8.7 %fusion.103 = bf16[256,2,768]{2,0,1:T(8,128)(2,1)S(1)} fusion(bf16[4096,2,768]{2,1,0:T(2,128)(2,1)} %bitcast.196, f32[4096]{0:T(1024)S(1)} %bitcast.192, f32[256]{0:T(256)S(1)} %get-tuple-element.77, bf16[512,4096]{1,0:T(8,128)(2,1)} %param.16), kind=kOutput, calls=%fused_computation.112 | convolution fusion | flops 3225812992 | bytes 15483904 | tf_op jit(solution)/shard_map/sd,dhe->she/dot_general | solution.py:43
  22.4 0.3 copy.53
  24.0 1.0 multiply_cosine_fusion.1
  24.9 0.2 fusion.150
  25.2 0.2 fusion.154
  25.5 1.0 maximum_select_fusion.1
  26.5 0.8 collective-permute-start
  27.3 2.7 collective-permute-start.3
  30.2 0.7 iota_compare_fusion.3
  31.1 8.6 %fusion.127 = bf16[8,2,1,6,128]{4,0,3,1,2:T(8,128)(2,1)S(1)} fusion(bf16[4096,2,768]{2,1,0:T(2,128)(2,1)} %bitcast.169, bf16[8,4096]{1,0:T(8,128)(2,1)S(1)} %copy-done.11, f32[4096]{0:T(1024)S(1)} %bitcast.188, f32[8]{0:T(128)S(1)} %add_rsqrt_fusion.5), kind=kOutput, calls=%fused_computation.130 | convolution fusion | flops 100806656 | bytes 12689440 | tf_op jit(solution)/shard_map/bd,dije->bije/dot_general | solution.py:105
  39.7 0.7 fusion.239
  40.7 20.6 %broadcast_select_fusion.3 = (bf16[8,768,2,128]{3,2,1,0:T(2,128)(2,1)}, bf16[8,768,2,128]{3,2,1,0:T(2,128)(2,1)}) fusion(pred[8,768]{1,0:T(8,128)(4,1)S(1)} %get-tuple-element.67, bf16[1,8,768,2,1,128]{5,3,4,2,1,0:T(2,128)(2,1)S(1)} %copy-done.2, bf16[8,2,128]{2,1,0:T(2,128)(2,1)S(1)} %copy.75, bf16[1,8,768,2,1,128]{5,3,4,2,1,0:T(2,128)(2,1)S(1)} %copy-done.3, ...), kind=kLoop, calls=%fused_computation.42 | loop fusion | flops 3145728 | bytes 12597248 | tf_op jit(solution)/shard_map/jit(_where)/select_n | solution.py:110
  61.4 20.6 %broadcast_select_fusion = (bf16[1,8,768,2,1,128]{5,3,4,2,1,0:T(2,128)(2,1)}, bf16[1,8,768,2,1,128]{5,3,4,2,1,0:T(2,128)(2,1)}) fusion(bf16[1,8,768,2,1,128]{5,3,4,2,1,0:T(2,128)(2,1)S(1)} %copy-done.3, pred[8,768]{1,0:T(8,128)(4,1)S(1)} %get-tuple-element.67, bf16[8,2,128]{2,1,0:T(2,128)(2,1)S(1)} %copy.77, ...), kind=kLoop, calls=%fused_computation.39 | loop fusion | flops 3145728 | bytes 12597248 | tf_op jit(solution)/shard_map/jit(_where)/select_n | solution.py:111
  82.0 0.3 copy.105
  82.2 0.3 copy.106
  82.7 1.4 fusion.138
  84.1 5.1 fusion.240
  89.3 2.9 fusion.113
  92.1 0.6 slice-done
  92.7 1.3 slice-done.1
  94.0 4.6 fusion.36
  98.5 0.3 copy.101
  98.8 0.3 copy.102
  99.2 0.3 fusion.134
  99.6 2.4 fusion.241
  102.0 1.9 convolution_convert_fusion
  104.0 8.0 %fusion.33 = f32[256,4096]{1,0:T(8,128)} fusion(bf16[256,2,512]{0,2,1:T(8,128)(2,1)S(1)} %bitcast.178, bf16[1,2,512,4096]{3,2,1,0:T(8,128)(2,1)} %param.23), kind=kOutput, calls=%fused_computation.45 | convolution fusion | flops 2147483648 | bytes 13107200 | tf_op jit(solution)/shard_map/qhf,hfd->qd/dot_general | solution.py:60
  112.0 3.6 fusion.246
  115.7 1.5 fusion.130
  117.2 4.7 fusion.42
  121.9 152.1 %all-reduce.4 = (bf16[256,4096]{1,0:T(8,128)(2,1)}, bf16[256,4096]{1,0:T(8,128)(2,1)}, bf16[8,4096]{1,0:T(8,128)(2,1)S(1)}) all-reduce(f32[256,4096]{1,0:T(8,128)} %fusion.36, f32[256,4096]{1,0:T(8,128)} %fusion.33, f32[8,4096]{1,0:T(8,128)S(1)} %fusion.42), channel_id=1, replica_groups=mesh['pair'=1,'tp'=4,'side'=8] {'tp'}, use_global_device_ids=true, to_apply=%region_9.10 | all-reduce | flops 2129920 | bytes 12779520 | tf_op jit(solution)/shard_map/psum | solution.py:161
  274.2 28.3 %fusion.39 = bf16[8,2,3584]{2,0,1:T(8,128)(2,1)S(1)} fusion(bf16[4096,2,3584]{2,1,0:T(2,128)(2,1)} %bitcast.166, bf16[8,4096]{1,0:T(8,128)(2,1)S(1)} %get-tuple-element.15, f32[4096]{0:T(1024)S(1)} %bitcast.183, f32[8]{0:T(128)S(1)} %add_rsqrt_fusion.4), kind=kOutput, calls=%fused_computation.51 | convolution fusion | flops 469950464 | bytes 58916896 | tf_op jit(solution)/shard_map/sd,dkf->skf/dot_general | solution.py:30
  302.5 11.5 %fusion.9 = f32[8,4096]{1,0:T(8,128)S(1)} fusion(bf16[1,3584,4096]{2,1,0:T(8,128)(2,1)} %param.30, bf16[8,2,3584]{2,0,1:T(8,128)(2,1)S(1)} %fusion.39), kind=kOutput, calls=%fused_computation.9 | convolution fusion | flops 235110400 | bytes 29605888 | tf_op jit(solution)/shard_map/dot_general | solution.py:32
  314.0 0.3 copy-done.10
  314.3 1.9 fusion.49
  316.3 36.2 %fusion.27 = bf16[256,2,3584]{2,0,1:T(8,128)(2,1)} fusion(bf16[4096,2,3584]{2,1,0:T(2,128)(2,1)} %bitcast.193, bf16[256,4096]{1,0:T(8,128)(2,1)S(1)} %get-tuple-element.17, f32[4096]{0:T(1024)S(1)} %bitcast.189, f32[256]{0:T(256)S(1)} %add_rsqrt_fusion.2), kind=kOutput, calls=%fused_computation.43 | convolution fusion | flops 15038414848 | bytes 64504832 | tf_op jit(solution)/shard_map/sd,dkf->skf/dot_general | solution.py:30
  352.5 16.2 %fusion.13 = f32[256,4096]{1,0:T(8,128)} fusion(bf16[1,3584,4096]{2,1,0:T(8,128)(2,1)} %param.25, bf16[256,2,3584]{2,0,1:T(8,128)(2,1)} %fusion.27), kind=kOutput, calls=%fused_computation.13 | convolution fusion | flops 7523532800 | bytes 37224448 | tf_op jit(solution)/shard_map/dot_general | solution.py:32
  368.7 35.2 %fusion.30 = bf16[256,2,3584]{2,0,1:T(8,128)(2,1)} fusion(bf16[4096,2,3584]{2,1,0:T(2,128)(2,1)} %bitcast.194, bf16[256,4096]{1,0:T(8,128)(2,1)S(1)} %get-tuple-element.21, f32[256]{0:T(256)S(1)} %add_rsqrt_fusion, f32[4096]{0:T(1024)S(1)} %bitcast.190), kind=kOutput, calls=%fused_computation.44 | convolution fusion | flops 15038414848 | bytes 64504832 | tf_op jit(solution)/shard_map/sd,dkf->skf/dot_general | solution.py:30
  403.9 16.1 %fusion.11 = f32[256,4096]{1,0:T(8,128)} fusion(bf16[1,3584,4096]{2,1,0:T(8,128)(2,1)} %param.25, bf16[256,2,3584]{2,0,1:T(8,128)(2,1)} %fusion.30), kind=kOutput, calls=%fused_computation.11 | convolution fusion | flops 7523532800 | bytes 37224448 | tf_op jit(solution)/shard_map/dot_general | solution.py:32
  420.0 146.5 %all-reduce.5 = (bf16[256,4096]{1,0:T(8,128)(2,1)}, bf16[256,4096]{1,0:T(8,128)(2,1)}, bf16[8,4096]{1,0:T(8,128)(2,1)S(1)}) all-reduce(f32[256,4096]{1,0:T(8,128)} %fusion.11, f32[256,4096]{1,0:T(8,128)} %fusion.13, f32[8,4096]{1,0:T(8,128)S(1)} %fusion.9), channel_id=1, replica_groups=mesh['pair'=1,'tp'=4,'side'=8] {'tp'}, use_global_device_ids=true, to_apply=%region_11.12 | all-reduce | flops 2129920 | bytes 12779520 | tf_op jit(solution)/shard_map/psum | solution.py:161
  566.6 3.2 fusion.52
  569.7 0.3 copy-done.8
  570.0 2.1 fusion.60
  572.2 0.6 fusion.171
  572.8 1.0 constant_dynamic-slice_fusion.2
  573.8 0.7 collective-permute-start.1
  574.5 3.0 collective-permute-start.2
  577.5 1.0 constant_dynamic-slice_fusion
  578.5 0.7 collective-permute-start.4
  579.1 2.0 collective-permute-start.5
  581.1 4.0 pad_maximum_fusion
  585.1 0.2 copy.81
  585.3 0.2 copy.82
  585.6 0.2 copy.83
  585.8 0.2 copy.84
  586.1 6.3 %dynamic_update_slice.16 = bf16[1,512,2,1,128]{4,2,3,1,0:T(2,128)(2,1)S(1)} dynamic-update-slice(bf16[1,512,2,1,128]{4,2,3,1,0:T(2,128)(2,1)S(1)} %broadcast_in_dim.140.clone, bf16[1,512,1,1,128]{4,2,3,1,0:T(2,128)(2,1)S(1)} %copy.81, s32[]{:T(128)} %constant.99.clone.1, s32[]{:T(128)} %constant.99.clone.1, s32[]{:T(128)S(6)} %select_n.120, s32[]{:T(128)} %constant.99.clone.1, s32[]{:T(128)} %constant.99.clone.1) | dynamic-update-slice | bytes 262148 | tf_op jit(solution)/shard_map/dynamic_update_slice | solution.py:138
  592.6 6.3 %dynamic_update_slice.18 = bf16[1,512,2,1,128]{4,2,3,1,0:T(2,128)(2,1)S(1)} dynamic-update-slice(bf16[1,512,2,1,128]{4,2,3,1,0:T(2,128)(2,1)S(1)} %broadcast_in_dim.140.clone.1, bf16[1,512,1,1,128]{4,2,3,1,0:T(2,128)(2,1)S(1)} %copy.83, s32[]{:T(128)} %constant.99.clone.1, s32[]{:T(128)} %constant.99.clone.1, s32[]{:T(128)S(6)} %select_n.120, s32[]{:T(128)} %constant.99.clone.1, s32[]{:T(128)} %constant.99.clone.1) | dynamic-update-slice | bytes 262148 | tf_op jit(solution)/shard_map/dynamic_update_slice | solution.py:138
  598.9 6.3 %dynamic_update_slice.17 = bf16[1,512,2,1,128]{4,2,3,1,0:T(2,128)(2,1)S(1)} dynamic-update-slice(bf16[1,512,2,1,128]{4,2,3,1,0:T(2,128)(2,1)S(1)} %dynamic_update_slice.16, bf16[1,512,1,1,128]{4,2,3,1,0:T(2,128)(2,1)S(1)} %copy.82, s32[]{:T(128)} %constant.99.clone.1, s32[]{:T(128)} %constant.99.clone.1, s32[]{:T(128)S(6)} %select_n.124, s32[]{:T(128)} %constant.99.clone.1, s32[]{:T(128)} %constant.99.clone.1) | dynamic-update-slice | bytes 262148 | tf_op jit(solution)/shard_map/dynamic_update_slice | solution.py:138
  605.3 6.3 %dynamic_update_slice.19 = bf16[1,512,2,1,128]{4,2,3,1,0:T(2,128)(2,1)S(1)} dynamic-update-slice(bf16[1,512,2,1,128]{4,2,3,1,0:T(2,128)(2,1)S(1)} %dynamic_update_slice.18, bf16[1,512,1,1,128]{4,2,3,1,0:T(2,128)(2,1)S(1)} %copy.84, s32[]{:T(128)} %constant.99.clone.1, s32[]{:T(128)} %constant.99.clone.1, s32[]{:T(128)S(6)} %select_n.124, s32[]{:T(128)} %constant.99.clone.1, s32[]{:T(128)} %constant.99.clone.1) | dynamic-update-slice | bytes 262148 | tf_op jit(solution)/shard_map/dynamic_update_slice | solution.py:138
  611.6 0.7 copy-done.18
  (102 shorter events, 2.2 us)
Async XLA Ops:
  0.6 4.7 copy-start
  22.7 7.5 %copy-start.29 = (s32[8]{0:T(128)S(1)}, s32[8]{0:T(128)}, u32[]{:S(2)}) copy-start(s32[8]{0:T(128)} %param.21) | copy-start | bytes 100
  22.7 8.2 %copy-start.20 = (bf16[1,2,4096]{2,1,0:T(2,128)(2,1)S(1)}, bf16[1,2,4096]{2,1,0:T(2,128)(2,1)}, u32[]{:S(2)}) copy-start(bf16[1,2,4096]{2,1,0:T(2,128)(2,1)} %param.31) | copy-start | bytes 49156
  22.7 8.2 %copy-start.11 = (bf16[8,4096]{1,0:T(8,128)(2,1)S(1)}, bf16[8,4096]{1,0:T(8,128)(2,1)}, u32[]{:S(2)}) copy-start(bf16[8,4096]{1,0:T(8,128)(2,1)} %param.18) | copy-start | bytes 196612
  23.8 6.3 %copy-start.14 = (bf16[256,2,1,128]{3,0,1,2:T(8,128)(2,1)}, bf16[256,2,1,128]{3,0,1,2:T(8,128)(2,1)S(1)}, u32[]{:S(2)}) copy-start(bf16[256,2,1,128]{3,0,1,2:T(8,128)(2,1)S(1)} %copy.99) | copy-start | bytes 393220
  23.9 6.2 %copy-start.16 = (bf16[256,2,1,128]{3,0,1,2:T(8,128)(2,1)}, bf16[256,2,1,128]{3,0,1,2:T(8,128)(2,1)S(1)}, u32[]{:S(2)}) copy-start(bf16[256,2,1,128]{3,0,1,2:T(8,128)(2,1)S(1)} %copy.103) | copy-start | bytes 393220
  25.4 2.0 copy-start.12
  25.4 4.7 copy-start.13
  26.5 546.3 %collective-permute-start = (bf16[1,512,2,128]{3,1,2,0:T(8,128)(2,1)}, bf16[1,512,2,128]{3,1,2,0:T(8,128)(2,1)}, u32[]{:S(2)}, u32[]{:S(2)}) collective-permute-start(bf16[1,512,2,128]{3,1,2,0:T(8,128)(2,1)} %get-tuple-element.65), channel_id=1, source_target_pairs={{0,4},{1,5},{2,6},{3,7},{4,0},{5,1},{6,2},{7,3},{8,12},{9,13},{10,... | collective-permute-start | bytes 786440 | tf_op jit(solution)/shard_map/ppermute | solution.py:144
  27.3 550.1 %collective-permute-start.3 = (bf16[1,512,2,128]{3,1,2,0:T(8,128)(2,1)}, bf16[1,512,2,128]{3,1,2,0:T(8,128)(2,1)}, u32[]{:S(2)}, u32[]{:S(2)}) collective-permute-start(bf16[1,512,2,128]{3,1,2,0:T(8,128)(2,1)} %get-tuple-element.64), channel_id=1, source_target_pairs={{0,4},{1,5},{2,6},{3,7},{4,0},{5,1},{6,2},{7,3},{8,12},{9,13},{10,... | collective-permute-start | bytes 786440 | tf_op jit(solution)/shard_map/ppermute | solution.py:144
  31.1 9.6 %copy-start.2 = (bf16[1,8,768,2,1,128]{5,3,4,2,1,0:T(2,128)(2,1)S(1)}, bf16[1,8,768,2,1,128]{5,3,4,2,1,0:T(2,128)(2,1)}, u32[]{:S(2)}) copy-start(bf16[1,8,768,2,1,128]{5,3,4,2,1,0:T(2,128)(2,1)} %param.19) | copy-start | bytes 9437188
  31.1 9.6 %copy-start.3 = (bf16[1,8,768,2,1,128]{5,3,4,2,1,0:T(2,128)(2,1)S(1)}, bf16[1,8,768,2,1,128]{5,3,4,2,1,0:T(2,128)(2,1)}, u32[]{:S(2)}) copy-start(bf16[1,8,768,2,1,128]{5,3,4,2,1,0:T(2,128)(2,1)} %param.20) | copy-start | bytes 9437188
  40.5 20.8 %copy-start.23 = (f32[8,64]{1,0:T(8,128)}, f32[8,64]{1,0:T(8,128)S(1)}, u32[]{:S(2)}) copy-start(f32[8,64]{1,0:T(8,128)S(1)} %get-tuple-element.62) | copy-start | bytes 6148
  40.5 20.8 %copy-start.25 = (f32[8,64]{1,0:T(8,128)}, f32[8,64]{1,0:T(8,128)S(1)}, u32[]{:S(2)}) copy-start(f32[8,64]{1,0:T(8,128)S(1)} %get-tuple-element.63) | copy-start | bytes 6148
  84.1 5.1 copy-start.15
  84.1 5.1 copy-start.17
  89.2 3.4 slice-start
  89.2 4.7 slice-start.1
  103.9 8.0 %copy-start.21 = (bf16[8,2,1,4,64]{4,0,3,1,2:T(8,128)(2,1)S(1)}, bf16[8,2,1,4,64]{4,0,3,1,2:T(8,128)(2,1)}, u32[]{:S(2)}) copy-start(bf16[8,2,1,4,64]{4,0,3,1,2:T(8,128)(2,1)} %get-tuple-element.44) | copy-start | bytes 24580
  103.9 8.0 %copy-start.22 = (bf16[8,2,1,4,64]{4,0,3,1,2:T(8,128)(2,1)S(1)}, bf16[8,2,1,4,64]{4,0,3,1,2:T(8,128)(2,1)}, u32[]{:S(2)}) copy-start(bf16[8,2,1,4,64]{4,0,3,1,2:T(8,128)(2,1)} %get-tuple-element.45) | copy-start | bytes 24580
  103.9 8.0 %copy-start.24 = (f32[8,64]{1,0:T(8,128)S(1)}, f32[8,64]{1,0:T(8,128)}, u32[]{:S(2)}) copy-start(f32[8,64]{1,0:T(8,128)} %copy-done.23) | copy-start | bytes 6148
  104.0 8.0 %copy-start.26 = (f32[8,64]{1,0:T(8,128)S(1)}, f32[8,64]{1,0:T(8,128)}, u32[]{:S(2)}) copy-start(f32[8,64]{1,0:T(8,128)} %copy-done.25) | copy-start | bytes 6148
  104.0 8.1 %copy-start.28 = (pred[8,768]{1,0:T(8,128)(4,1)S(1)}, pred[8,768]{1,0:T(8,128)(4,1)}, u32[]{:S(2)}) copy-start(pred[8,768]{1,0:T(8,128)(4,1)} %get-tuple-element.66) | copy-start | bytes 18436
  104.0 11.7 %copy-start.7 = (bf16[8,768,2,128]{3,2,1,0:T(2,128)(2,1)S(1)}, bf16[8,768,2,128]{3,2,1,0:T(2,128)(2,1)}, u32[]{:S(2)}) copy-start(bf16[8,768,2,128]{3,2,1,0:T(2,128)(2,1)} %get-tuple-element.57) | copy-start | bytes 9437188
  302.5 11.5 %copy-start.1 = (bf16[512,4096]{1,0:T(8,128)(2,1)S(1)}, bf16[512,4096]{1,0:T(8,128)(2,1)}, u32[]{:S(2)}) copy-start(bf16[512,4096]{1,0:T(8,128)(2,1)} %param.16) | copy-start | bytes 12582916
  302.5 11.5 %copy-start.9 = (bf16[256,4096]{1,0:T(8,128)(2,1)S(1)}, bf16[256,4096]{1,0:T(8,128)(2,1)}, u32[]{:S(2)}) copy-start(bf16[256,4096]{1,0:T(8,128)(2,1)} %get-tuple-element.11) | copy-start | bytes 6291460
  302.5 11.8 %copy-start.10 = (bf16[256,4096]{1,0:T(8,128)(2,1)S(1)}, bf16[256,4096]{1,0:T(8,128)(2,1)}, u32[]{:S(2)}) copy-start(bf16[256,4096]{1,0:T(8,128)(2,1)} %get-tuple-element.12) | copy-start | bytes 6291460
  314.3 2.0 copy-start.27
  316.2 36.2 %copy-start.6 = (bf16[256,4096]{1,0:T(8,128)(2,1)}, bf16[256,4096]{1,0:T(8,128)(2,1)S(1)}, u32[]{:S(2)}) copy-start(bf16[256,4096]{1,0:T(8,128)(2,1)S(1)} %get-tuple-element.17) | copy-start | bytes 6291460
  316.2 52.4 %copy-start.4 = (bf16[256,4096]{1,0:T(8,128)(2,1)}, bf16[256,4096]{1,0:T(8,128)(2,1)S(1)}, u32[]{:S(2)}) copy-start(bf16[256,4096]{1,0:T(8,128)(2,1)S(1)} %get-tuple-element.21) | copy-start | bytes 6291460
  566.6 3.2 copy-start.5
  566.6 3.5 copy-start.8
  573.8 11.3 %collective-permute-start.1 = (bf16[1,512,1,128]{3,1,2,0:T(8,128)(2,1)S(1)}, bf16[1,512,1,128]{3,1,2,0:T(8,128)(2,1)S(1)}, u32[]{:S(2)}, u32[]{:S(2)}) collective-permute-start(bf16[1,512,1,128]{3,1,2,0:T(8,128)(2,1)S(1)} %get-tuple-element.41), channel_id=1, source_target_pairs={{0,0},{8,16},{16,8},{24,24},{1,1},{9,17},{17,9},{25,25},{2,2},{10,... | collective-permute-start | bytes 393224 | tf_op jit(solution)/shard_map/ppermute | solution.py:137
  574.5 10.8 %collective-permute-start.2 = (bf16[1,512,1,128]{3,1,2,0:T(8,128)(2,1)S(1)}, bf16[1,512,1,128]{3,1,2,0:T(8,128)(2,1)S(1)}, u32[]{:S(2)}, u32[]{:S(2)}) collective-permute-start(bf16[1,512,1,128]{3,1,2,0:T(8,128)(2,1)S(1)} %get-tuple-element.40), channel_id=1, source_target_pairs={{0,8},{8,24},{16,0},{24,16},{1,9},{9,25},{17,1},{25,17},{2,10},{10... | collective-permute-start | bytes 393224 | tf_op jit(solution)/shard_map/ppermute | solution.py:137
  578.5 7.1 %collective-permute-start.4 = (bf16[1,512,1,128]{3,1,2,0:T(8,128)(2,1)S(1)}, bf16[1,512,1,128]{3,1,2,0:T(8,128)(2,1)S(1)}, u32[]{:S(2)}, u32[]{:S(2)}) collective-permute-start(bf16[1,512,1,128]{3,1,2,0:T(8,128)(2,1)S(1)} %get-tuple-element.39), channel_id=1, source_target_pairs={{0,0},{8,16},{16,8},{24,24},{1,1},{9,17},{17,9},{25,25},{2,2},{10,... | collective-permute-start | bytes 393224 | tf_op jit(solution)/shard_map/ppermute | solution.py:137
  579.1 6.6 %collective-permute-start.5 = (bf16[1,512,1,128]{3,1,2,0:T(8,128)(2,1)S(1)}, bf16[1,512,1,128]{3,1,2,0:T(8,128)(2,1)S(1)}, u32[]{:S(2)}, u32[]{:S(2)}) collective-permute-start(bf16[1,512,1,128]{3,1,2,0:T(8,128)(2,1)S(1)} %get-tuple-element.38), channel_id=1, source_target_pairs={{0,8},{8,24},{16,0},{24,16},{1,9},{9,25},{17,1},{25,17},{2,10},{10... | collective-permute-start | bytes 393224 | tf_op jit(solution)/shard_map/ppermute | solution.py:137
  605.3 6.4 %copy-start.19 = (bf16[1,512,2,1,128]{4,2,3,1,0:T(2,128)(2,1)}, bf16[1,512,2,1,128]{4,2,3,1,0:T(2,128)(2,1)S(1)}, u32[]{:S(2)}) copy-start(bf16[1,512,2,1,128]{4,2,3,1,0:T(2,128)(2,1)S(1)} %dynamic_update_slice.17) | copy-start | bytes 786436
  611.6 0.7 copy-start.18
where the time goes:
time: 620 us; the launch traced here: 612 us
  blocking collectives  299 us (48%)
  matrix products  204 us (33%)
  other arithmetic  63.7 us (10%)
  local copies, waits for them, and re-layouts  34.6 us (6%)
  starting transfers between devices  9.8 us (2%)
    psum x2, blocking collectives, tp_sum(): return lax.psum(part_sum, 'tp')  299 us
    dot_general x3, matrix products, mlp_block(): jnp.einsum('sd,dkf->skf', normed, w_ug, preferred_element_type=jnp.float32)  99.8 us
    dot_general x3, matrix products, mlp_block(): jnp.dot(act_out, w_down, preferred_element_type=jnp.float32)  43.8 us
    dynamic_update_slice x4, local copies, waits for them, and re-layouts, tp_relayout(): lax.dynamic_update_slice_in_dim(gathered, received, (dst_pos - round_idx)...  25.3 us
    select_n x1, other arithmetic, decode_side(): key_upd = jnp.where(write_slot, key_new[:, None], k_cache[layer_idx])  20.6 us
    select_n x1, other arithmetic, decode_side(): val_upd = jnp.where(write_slot, val_new[:, None], v_cache[layer_idx])  20.6 us
    dot_general x2, matrix products, prompt_layer(): jnp.einsum('sd,dhe->she', normed, w_qkv, preferred_element_type=jnp.float32)  16.7 us
    dot_general x2, matrix products, prompt_layer(): jnp.einsum('qhf,hfd->qd', attn_out.reshape(num_rows, kv_loc, group * head...  12.6 us
  transfers between devices with their start and end apart: 6, of which 0 were waited for; matrix products, arithmetic and copies ran while one was open for 40% of the time, Pallas kernels for 0%

commit v1 on v0

v1 whole, which is shorter than its diff:
```python
import jax
import jax.numpy as jnp
from jax import lax
from jax.experimental import pallas as pl
from jax.experimental.pallas import tpu as pltpu
from jax.sharding import PartitionSpec as P

ROPE_BASE = 10000.0
NORM_EPS = 1e-5
F32 = jnp.float32
BF16 = jnp.bfloat16


def rms_norm(hidden, gain):
    val_f32 = hidden.astype(F32)
    inv_rms = lax.rsqrt(jnp.mean(val_f32 * val_f32, axis=-1, keepdims=True) + NORM_EPS)
    return (val_f32 * inv_rms * gain.astype(F32)).astype(BF16)


def rope_rot(vals_in, positions):
    half_dim = vals_in.shape[-1] // 2
    inv_freq = ROPE_BASE ** (-jnp.arange(half_dim, dtype=F32) / half_dim)
    angles = positions.astype(F32)[:, None] * inv_freq[None, :]
    tab_shape = (angles.shape[0],) + (1,) * (vals_in.ndim - 2) + (half_dim,)
    cos_tab = jnp.cos(angles).reshape(tab_shape)
    sin_tab = jnp.sin(angles).reshape(tab_shape)
    lo_half = vals_in[..., :half_dim].astype(F32)
    hi_half = vals_in[..., half_dim:].astype(F32)
    return jnp.concatenate([lo_half * cos_tab - hi_half * sin_tab, hi_half * cos_tab + lo_half * sin_tab], axis=-1).astype(BF16)


def residual(hidden, delta_f32):
    return (hidden.astype(F32) + delta_f32.astype(BF16).astype(F32)).astype(BF16)


def up_act(normed, w_ug):
    upgate = jnp.einsum('sd,dkf->skf', normed, w_ug, preferred_element_type=F32).astype(BF16)
    return (jax.nn.silu(upgate[:, 1].astype(F32)) * upgate[:, 0].astype(F32)).astype(BF16)


def ring_maps(tp_size):
    fwd = [(i, (i + 1) % tp_size) for i in range(tp_size)]
    bwd = [(i, (i - 1) % tp_size) for i in range(tp_size)]
    return fwd, bwd


def ring_reduce_scatter(part, tp_size):
    fwd, bwd = ring_maps(tp_size)
    rows = part.shape[0] // tp_size
    half = rows // 2
    blk = [part[j * rows:(j + 1) * rows] for j in range(tp_size)]
    got_f = lax.ppermute(jnp.concatenate([blk[2][:half], blk[1][half:]]), 'tp', fwd)
    got_b = lax.ppermute(jnp.concatenate([blk[3][:half], blk[2][half:]]), 'tp', bwd)
    last_f = lax.ppermute(blk[1][:half] + got_f[:half], 'tp', fwd)
    last_b = lax.ppermute(blk[3][half:] + got_b[half:], 'tp', bwd)
    top = blk[0][:half] + (last_f + got_b[:half])
    bot = blk[0][half:] + (got_f[half:] + last_b)
    return jnp.concatenate([top, bot])


def ring_all_gather(own, tp_size):
    fwd, bwd = ring_maps(tp_size)
    half = own.shape[0] // 2
    prev_blk = lax.ppermute(own, 'tp', fwd)
    next_blk = lax.ppermute(own, 'tp', bwd)
    far_top = lax.ppermute(prev_blk[:half], 'tp', fwd)
    far_bot = lax.ppermute(next_blk[half:], 'tp', bwd)
    return [own, next_blk, jnp.concatenate([far_top, far_bot]), prev_blk]


def roll_rows(vals, start):
    return lax.dynamic_slice_in_dim(jnp.concatenate([vals, vals]), start, vals.shape[0], axis=0)


def prompt_attention(x_rows, seq_len, w_qkv, head_dim, group, gain, half_len):
    num_rows = x_rows.shape[0]
    kv_loc = w_qkv.shape[1]
    positions = jnp.arange(num_rows)
    normed = rms_norm(x_rows, gain)
    qkv_all = jnp.einsum('sd,dhe->she', normed, w_qkv, preferred_element_type=F32).astype(BF16)
    qkv_all = qkv_all.reshape(num_rows, kv_loc, group + 2, head_dim)
    queries = rope_rot(qkv_all[:, :, :group], positions)
    key_all = rope_rot(qkv_all[:, :, group], positions)
    val_all = qkv_all[:, :, group + 1]
    outs = []
    for q_start in range(0, num_rows, half_len):
        k_end = q_start + half_len
        key_pos = jnp.arange(k_end)
        allowed = (key_pos[None, :] <= positions[q_start:k_end, None]) & (key_pos[None, :] < seq_len)
        scores = jnp.einsum('qhgd,khd->hgqk', queries[q_start:k_end], key_all[:k_end], preferred_element_type=F32) * head_dim ** -0.5
        scores = jnp.where(allowed, scores, -1e30)
        attn_prob = jax.nn.softmax(scores, axis=-1).astype(BF16)
        attn_out = jnp.einsum('hgqk,khd->qhgd', attn_prob, val_all[:k_end], preferred_element_type=F32).astype(BF16)
        outs.append(attn_out.reshape(half_len, kv_loc * group * head_dim))
    valid = (positions < seq_len)[:, None, None]
    zero_val = jnp.zeros((), BF16)
    return outs, jnp.where(valid, key_all, zero_val), jnp.where(valid, val_all, zero_val)


def hand_off(key_cache, val_cache, tp_size, side_size):
    t_idx = lax.axis_index('tp')
    both = jnp.stack([key_cache, val_cache])
    head0, head1 = both[:, :, 0], both[:, :, 1]
    low = t_idx < tp_size // 2
    received = []
    for rnd in range(2):
        piece = jnp.where(low, head1, head0) if rnd else jnp.where(low, head0, head1)
        pairs = []
        for t in range(tp_size):
            for s in range(side_size):
                dst_t = (t % 2) * 2 + (rnd + t // 2) % 2
                pairs.append((t * side_size + s, dst_t * side_size + (s + side_size // 2) % side_size))
        received.append(lax.ppermute(piece, ('tp', 'side'), pairs))
    even = t_idx % 2 == 0
    slot0 = jnp.where(even, received[0], received[1])
    slot1 = jnp.where(even, received[1], received[0])
    out = jnp.stack([slot0, slot1], axis=2)
    return out[0][None, :, :, None], out[1][None, :, :, None]


def cache_kernel(len_ref, kc_ref, vc_ref, kn_ref, vn_ref, ko_ref, vo_ref):
    slot = len_ref[pl.program_id(0)]
    ko_ref[...] = kc_ref[...]
    vo_ref[...] = vc_ref[...]
    ko_ref[0, pl.ds(slot, 1)] = kn_ref[...]
    vo_ref[0, pl.ds(slot, 1)] = vn_ref[...]


def cache_update(lengths, k_cache, v_cache, key_new, val_new):
    rows, slots, kv_loc, dim = k_cache.shape
    big = pl.BlockSpec((1, slots, kv_loc, dim), lambda b, lens: (b, 0, 0, 0))
    small = pl.BlockSpec((1, kv_loc, dim), lambda b, lens: (b, 0, 0))
    shape = jax.ShapeDtypeStruct(k_cache.shape, k_cache.dtype)
    return pl.pallas_call(
        cache_kernel,
        grid_spec=pltpu.PrefetchScalarGridSpec(num_scalar_prefetch=1, grid=(rows,), in_specs=[big, big, small, small], out_specs=[big, big]),
        out_shape=[shape, shape],
        cost_estimate=pl.CostEstimate(flops=10 ** 9, bytes_accessed=4 * k_cache.size * 2, transcendentals=0),
        name='cache_update',
    )(lengths, k_cache, v_cache, key_new, val_new)


def decode_side(tokens, lengths, k_cache, v_cache, w_qkv, w_out, w_ug, w_down, gains):
    batch_rows = tokens.shape[0]
    kv_loc = w_qkv.shape[1]
    head_dim = (w_qkv.shape[2] - w_out.shape[1]) // 2
    group = w_out.shape[1] // head_dim
    visible = (jnp.arange(k_cache.shape[1])[None, :] <= lengths[:, None])[:, None, None, :]
    normed = rms_norm(tokens, gains[0])
    qkv_all = jnp.einsum('bd,die->bie', normed, w_qkv, preferred_element_type=F32).astype(BF16)
    qkv_all = qkv_all.reshape(batch_rows, kv_loc, group + 2, head_dim)
    queries = rope_rot(qkv_all[:, :, :group], lengths)
    key_new = rope_rot(qkv_all[:, :, group], lengths)
    val_new = qkv_all[:, :, group + 1]
    key_upd, val_upd = cache_update(lengths, k_cache, v_cache, key_new, val_new)
    scores = jnp.einsum('bige,bsie->bigs', queries, key_upd, preferred_element_type=F32) * head_dim ** -0.5
    scores = jnp.where(visible, scores, -1e30)
    attn_prob = jax.nn.softmax(scores, axis=-1).astype(BF16)
    attn_out = jnp.einsum('bigs,bsie->bige', attn_prob, val_upd, preferred_element_type=F32).astype(BF16)
    attn_proj = lax.psum(jnp.einsum('bif,ifd->bd', attn_out.reshape(batch_rows, kv_loc, group * head_dim), w_out, preferred_element_type=F32), 'tp')
    hidden = residual(tokens, attn_proj)
    act = up_act(rms_norm(hidden, gains[1]), w_ug)
    hidden = residual(hidden, lax.psum(jnp.dot(act, w_down, preferred_element_type=F32), 'tp'))
    return hidden, key_upd, val_upd


def solution(mesh):
    tp_size = mesh.shape['tp']
    side_size = mesh.shape['side']
    rows_spec = P(('pair', 'side'), None)
    flat_spec = P(('pair', 'side'))
    cache_spec = P(None, ('pair', 'side'), None, None, 'tp', None)
    prompt_spec = P(None, ('pair', 'side'), None, 'tp', None)
    in_specs = (rows_spec, flat_spec, rows_spec, cache_spec, cache_spec, flat_spec,
                P(None, None, 'tp', None), P(None, 'tp', None, None), P(None, None, None, 'tp'), P(None, 'tp', None), P(),
                P(None, None, None, 'tp', None), P(None, None, 'tp', None, None), P(None, None, None, 'tp'), P(None, 'tp', None), P())
    out_specs = (rows_spec, rows_spec, prompt_spec, prompt_spec, cache_spec, cache_spec)

    def body(x_prompt, s_len, y_tok, k_cache, v_cache, c_len, wqkv_a, wo_a, wug_a, wd_a, norm_a, wqkv_b, wo_b, wug_b, wd_b, norm_b):
        t_idx = lax.axis_index('tp')
        half_len = x_prompt.shape[0] // 2
        blk = half_len // tp_size
        head_dim = (wqkv_a.shape[3] - wo_a.shape[2]) // 2
        group = wo_a.shape[2] // head_dim
        w_out = wo_a[0].reshape(-1, wo_a.shape[3])
        attn, key_cache, val_cache = prompt_attention(x_prompt, s_len[0], wqkv_a[0], head_dim, group, norm_a[0, 0], half_len)
        own_h, normed = [], []
        for idx in range(2):
            part = jnp.dot(roll_rows(attn[idx], t_idx * blk), w_out, preferred_element_type=F32)
            own = lax.dynamic_slice_in_dim(x_prompt, idx * half_len + t_idx * blk, blk, axis=0)
            own = residual(own, ring_reduce_scatter(part, tp_size))
            own_h.append(own)
            normed.append(jnp.concatenate(ring_all_gather(rms_norm(own, norm_a[0, 1]), tp_size)))
        k_prompt, v_prompt = hand_off(key_cache, val_cache, tp_size, side_size)
        hidden = jnp.zeros_like(x_prompt)
        for idx in range(2):
            act = up_act(normed[idx], wug_a[0])
            part = jnp.dot(act, wd_a[0], preferred_element_type=F32)
            own = residual(own_h[idx], ring_reduce_scatter(part, tp_size))
            for j, rows in enumerate(ring_all_gather(own, tp_size)):
                hidden = lax.dynamic_update_slice_in_dim(hidden, rows, idx * half_len + lax.rem(t_idx + j, tp_size) * blk, axis=0)
        kc = k_cache[0, :, :, :, 0]
        vc = v_cache[0, :, :, :, 0]
        y_out, k_new, v_new = decode_side(y_tok, c_len, kc, vc, wqkv_b[0, :, :, 0], wo_b[0, :, 0], wug_b[0], wd_b[0], norm_b[0])
        return hidden, y_out, k_prompt, v_prompt, k_new[None, :, :, :, None], v_new[None, :, :, :, None]

    return jax.shard_map(body, mesh=mesh, in_specs=in_specs, out_specs=out_specs, check_vma=False)
```

time: 620 us -> 484 us (0.78)
  the two profiles are of different devices: /device:TPU:100 before, /device:TPU:96 now
where the time goes in v1:
time: 484 us; the launch traced here: 475 us
  matrix products  192 us (40%)
  waiting for transfers between devices  110 us (23%)
  starting transfers between devices  51.5 us (11%)
  blocking collectives  45.5 us (9%)
  other arithmetic  41.8 us (9%)
  local copies, waits for them, and re-layouts  22.9 us (5%)
  Pallas kernels  8.44 us (2%)
    dot_general x3, matrix products, up_act(): jnp.einsum('sd,dkf->skf', normed, w_ug, preferred_element_type=F32)  99.1 us
    ppermute x4, waiting for transfers between devices, ring_reduce_scatter(): lax.ppermute(jnp.concatenate([blk[2][:half], blk[1][half:]]), 'tp', fwd)  41.6 us
    dot_general x2, matrix products, body(): part = jnp.dot(act, wd_a[0], preferred_element_type=F32)  31.1 us
    psum x1, blocking collectives, decode_side(): lax.psum(jnp.dot(act, w_down, preferred_element_type=F32), 'tp')  28.5 us
    ppermute x4, waiting for transfers between devices, ring_all_gather(): prev_blk = lax.ppermute(own, 'tp', fwd)  24.7 us
    ppermute x4, waiting for transfers between devices, ring_reduce_scatter(): last_b = lax.ppermute(blk[3][half:] + got_b[half:], 'tp', bwd)  18.3 us
    psum x1, blocking collectives, decode_side(): lax.psum(jnp.einsum('bif,ifd->bd', attn_out.reshape(batch_rows, kv_loc, g...  17 us
    unnamed x38, local copies, waits for them, and re-layouts  16.2 us
  transfers between devices with their start and end apart: 34, of which 15 were waited for; matrix products, arithmetic and copies ran while one was open for 44% of the time, Pallas kernels for 2%

profile of v1, /device:TPU:96, one launch (start us, length us, event | category | flops | bytes accessed | tf_op | source)
XLA Modules:
  0.0 474.8 jit_solution(15934818863899321244)
XLA Ops:
  1.6 3.3 fusion.19
  4.9 10.7 %fusion.70 = bf16[512,2,768]{2,0,1:T(8,128)(2,1)S(1)} fusion(bf16[4096,2,768]{2,1,0:T(2,128)(2,1)} %bitcast.187, bf16[512,4096]{1,0:T(8,128)(2,1)S(1)} %copy-done.2, f32[4096]{0:T(1024)S(1)} %bitcast.184, f32[512]{0:T(512)S(1)} %add_rsqrt_fusion), kind=kOutput, calls=%fused_computation.75 | convolution fusion | flops 6451625984 | bytes 18368512 | tf_op jit(solution)/shard_map/sd,dhe->she/dot_general | solution.py:80
  22.9 3.2 fusion.58
  26.3 3.5 fusion.225
  29.8 1.9 convolution_convert_fusion
  31.7 6.0 %fusion.111 = f32[256,4096]{1,0:T(8,128)S(1)} fusion(bf16[1024,4096]{1,0:T(8,128)(2,1)} %bitcast.165, s32[]{:T(128)S(6)} %select_n.100, bf16[256,1024]{0,1:T(8,128)(2,1)S(1)} %bitcast.179), kind=kOutput, calls=%fused_computation.129 | convolution fusion | flops 2148532224 | bytes 13107204 | tf_op jit(solution)/shard_map/dot_general | solution.py:189
  37.7 2.0 copy-done
  40.8 1.7 collective-permute-start
  42.7 5.0 %fusion.224 = (f32[2,4,256]{2,1,0:T(4,128)S(1)}, f32[2,4,256,512]{2,3,1,0:T(8,128)}) fusion(pred[256,512]{0,1:T(8,128)(4,1)S(1)} %fusion.132, bf16[512,2,64]{2,0,1:T(8,128)(2,1)S(1)} %get-tuple-element.78, bf16[512,2,64]{2,0,1:T(8,128)(2,1)S(1)} %get-tuple-element.79, bf16[512,2,4,64]{3,0,2,1:T(8,128)(2,1)} %get-tuple-element.72, ...), kind=kOutput, calls=%fused_computation.309 | convolution fusion | flops 274203136 | bytes 5644288 | tf_op jit(solution)/shard_map/sub | solution.py:92
  47.7 2.8 fusion.75
  52.4 2.6 fusion.108
  55.0 2.0 copy-done.1
  58.2 2.1 collective-permute-start.16
  61.5 3.3 collective-permute-start.32
  65.0 7.9 %fusion.86 = bf16[8,2,768]{2,0,1:T(8,128)(2,1)S(1)} fusion(bf16[4096,2,768]{2,1,0:T(2,128)(2,1)} %bitcast.169, bf16[8,4096]{1,0:T(8,128)(2,1)S(1)} %copy-done.7, f32[4096]{0:T(1024)S(1)} %bitcast.183, f32[8]{0:T(128)S(1)} %add_rsqrt_fusion.2), kind=kOutput, calls=%fused_computation.89 | convolution fusion | flops 100806656 | bytes 12689440 | tf_op jit(solution)/shard_map/bd,die->bie/dot_general | solution.py:150
  74.7 8.4 %cache_update.1 = (bf16[8,768,2,128]{3,2,1,0:T(2,128)(2,1)}, bf16[8,768,2,128]{3,2,1,0:T(2,128)(2,1)}) custom-call(s32[8]{0:T(128)} %len_ref.1, bf16[8,768,2,128]{3,2,1,0:T(2,128)(2,1)} %bitcast.174, bf16[8,768,2,128]{3,2,1,0:T(2,128)(2,1)} %bitcast.175, bf16[8,2,128]{2,1,0:T(2,128)(2,1)} %pad_maximum_fusion.11.kn_ref, ...), custom_call_target="tpu_custom_call" | custom-call | flops 1000000000 | bytes 12582912 | tf_op jit(solution)/shard_map/cache_update/pallas_call | solution.py:134
  83.1 3.0 fusion.230
  86.1 2.5 fusion.89
  88.6 4.6 fusion.33
  93.2 17.0 %all-reduce.2 = bf16[8,4096]{1,0:T(8,128)(2,1)S(1)} all-reduce(f32[8,4096]{1,0:T(8,128)S(1)} %fusion.33), channel_id=1, replica_groups=mesh['pair'=1,'tp'=4,'side'=8] {'tp'}, use_global_device_ids=true, to_apply=%region_10.11 | all-reduce | flops 32768 | bytes 196608 | tf_op jit(solution)/shard_map/psum | solution.py:160
  112.9 2.0 collective-permute-start.2
  115.3 2.3 slice_add_fusion.7
  118.7 2.8 collective-permute-start.18
  121.5 28.3 %fusion.30 = bf16[8,2,3584]{2,0,1:T(8,128)(2,1)S(1)} fusion(bf16[4096,2,3584]{2,1,0:T(2,128)(2,1)} %bitcast.164, bf16[8,4096]{1,0:T(8,128)(2,1)S(1)} %get-tuple-element.29, f32[4096]{0:T(1024)S(1)} %bitcast.181, f32[8]{0:T(128)S(1)} %add_rsqrt_fusion.1), kind=kOutput, calls=%fused_computation.32 | convolution fusion | flops 469950464 | bytes 58916896 | tf_op jit(solution)/shard_map/sd,dkf->skf/dot_general | solution.py:37
  149.9 1.8 fusion.131
  151.7 3.3 collective-permute-start.3
  155.0 5.3 %collective-permute-done.17 = f32[32,4096]{1,0:T(8,128)S(1)} collective-permute-done((f32[32,4096]{1,0:T(8,128)}, f32[32,4096]{1,0:T(8,128)S(1)}, u32[]{:S(2)}, u32[]{:S(2)}) %collective-permute-start.17) | collective-permute-done | bytes 524320 | tf_op jit(solution)/shard_map/ppermute | solution.py:54
  160.2 1.6 collective-permute-done.18
  161.8 1.7 fusion.123
  163.5 2.9 collective-permute-start.19
  166.4 6.7 %collective-permute-done.3 = f32[32,4096]{1,0:T(8,128)S(1)} collective-permute-done((f32[32,4096]{1,0:T(8,128)S(1)}, f32[32,4096]{1,0:T(8,128)S(1)}, u32[]{:S(2)}, u32[]{:S(2)}) %collective-permute-start.3) | collective-permute-done | bytes 524320 | tf_op jit(solution)/shard_map/ppermute | solution.py:55
  174.2 5.6 %collective-permute-done.19 = f32[32,4096]{1,0:T(8,128)S(1)} collective-permute-done((f32[32,4096]{1,0:T(8,128)S(1)}, f32[32,4096]{1,0:T(8,128)S(1)}, u32[]{:S(2)}, u32[]{:S(2)}) %collective-permute-start.19) | collective-permute-done | bytes 524320 | tf_op jit(solution)/shard_map/ppermute | solution.py:55
  180.9 1.7 fusion.96
  182.6 1.6 constant_dynamic-update-slice_fusion.9
  184.1 1.7 collective-permute-start.20
  186.2 11.3 %fusion.9 = f32[8,4096]{1,0:T(8,128)S(1)} fusion(bf16[1,3584,4096]{2,1,0:T(8,128)(2,1)} %param.30, bf16[8,2,3584]{2,0,1:T(8,128)(2,1)S(1)} %fusion.30), kind=kOutput, calls=%fused_computation.9 | convolution fusion | flops 235110400 | bytes 29605888 | tf_op jit(solution)/shard_map/dot_general | solution.py:163
  197.5 3.3 collective-permute-start.4
  201.6 3.3 collective-permute-start.22
  204.9 12.7 %collective-permute-done.5 = bf16[64,4096]{1,0:T(8,128)(2,1)S(1)} collective-permute-done((bf16[64,4096]{1,0:T(8,128)(2,1)}, bf16[64,4096]{1,0:T(8,128)(2,1)S(1)}, u32[]{:S(2)}, u32[]{:S(2)}) %collective-permute-start.5) | collective-permute-done | bytes 524320 | tf_op jit(solution)/shard_map/ppermute | solution.py:64
  218.4 2.0 collective-permute-start.6
  225.5 35.7 %fusion.27 = bf16[256,2,3584]{2,0,1:T(8,128)(2,1)} fusion(bf16[4096,2,3584]{2,1,0:T(2,128)(2,1)} %bitcast.185, bf16[256,4096]{1,0:T(8,128)(2,1)} %constant_dynamic-update-slice_fusion.5), kind=kOutput, calls=%fused_computation.27 | convolution fusion | flops 15034220544 | bytes 64487424 | tf_op jit(solution)/shard_map/sd,dkf->skf/dot_general | solution.py:37
  261.3 35.2 %fusion.24 = bf16[256,2,3584]{2,0,1:T(8,128)(2,1)} fusion(bf16[4096,2,3584]{2,1,0:T(2,128)(2,1)} %bitcast.186, bf16[256,4096]{1,0:T(8,128)(2,1)S(1)} %constant_dynamic-update-slice_fusion), kind=kOutput, calls=%fused_computation.26 | convolution fusion | flops 15034220544 | bytes 64487424 | tf_op jit(solution)/shard_map/sd,dkf->skf/dot_general | solution.py:37
  296.4 14.8 %fusion.11 = f32[256,4096]{1,0:T(8,128)S(1)} fusion(bf16[1,3584,4096]{2,1,0:T(8,128)(2,1)} %param.25, bf16[256,2,3584]{2,0,1:T(8,128)(2,1)} %fusion.27), kind=kOutput, calls=%fused_computation.11 | convolution fusion | flops 7523532800 | bytes 37224448 | tf_op jit(solution)/shard_map/dot_general | solution.py:198
  311.3 16.3 %fusion.13 = f32[256,4096]{1,0:T(8,128)S(1)} fusion(bf16[1,3584,4096]{2,1,0:T(8,128)(2,1)} %param.25, bf16[256,2,3584]{2,0,1:T(8,128)(2,1)} %fusion.24), kind=kOutput, calls=%fused_computation.13 | convolution fusion | flops 7523532800 | bytes 37224448 | tf_op jit(solution)/shard_map/dot_general | solution.py:198
  328.6 26.5 %collective-permute-done.8 = f32[64,4096]{1,0:T(8,128)S(1)} collective-permute-done((f32[64,4096]{1,0:T(8,128)S(1)}, f32[64,4096]{1,0:T(8,128)S(1)}, u32[]{:S(2)}, u32[]{:S(2)}) %collective-permute-start.8) | collective-permute-done | bytes 1048608 | tf_op jit(solution)/shard_map/ppermute | solution.py:52
  357.1 2.0 collective-permute-start.9
  359.2 15.1 %collective-permute-done.24 = f32[64,4096]{1,0:T(8,128)S(1)} collective-permute-done((f32[64,4096]{1,0:T(8,128)S(1)}, f32[64,4096]{1,0:T(8,128)S(1)}, u32[]{:S(2)}, u32[]{:S(2)}) %collective-permute-start.24) | collective-permute-done | bytes 1048608 | tf_op jit(solution)/shard_map/ppermute | solution.py:52
  376.2 1.7 collective-permute-start.26
  378.0 28.5 %all-reduce.3 = bf16[8,4096]{1,0:T(8,128)(2,1)S(1)} all-reduce(f32[8,4096]{1,0:T(8,128)S(1)} %fusion.9), channel_id=1, replica_groups=mesh['pair'=1,'tp'=4,'side'=8] {'tp'}, use_global_device_ids=true, to_apply=%region_12.13 | all-reduce | flops 32768 | bytes 196608 | tf_op jit(solution)/shard_map/psum | solution.py:163
  406.6 1.8 fusion.127
  408.4 3.3 collective-permute-start.11
  411.7 7.9 %collective-permute-done.25 = f32[32,4096]{1,0:T(8,128)S(1)} collective-permute-done((f32[32,4096]{1,0:T(8,128)}, f32[32,4096]{1,0:T(8,128)S(1)}, u32[]{:S(2)}, u32[]{:S(2)}) %collective-permute-start.25) | collective-permute-done | bytes 524320 | tf_op jit(solution)/shard_map/ppermute | solution.py:54
  419.6 1.6 fusion.119
  421.7 2.3 collective-permute-done.11
  425.8 3.8 collective-permute-start.12
  429.6 3.8 collective-permute-done.27
  434.5 5.5 %collective-permute-done.13 = bf16[64,4096]{1,0:T(8,128)(2,1)S(1)} collective-permute-done((bf16[64,4096]{1,0:T(8,128)(2,1)S(1)}, bf16[64,4096]{1,0:T(8,128)(2,1)S(1)}, u32[]{:S(2)}, u32[]{:S(2)}) %collective-permute-start.13) | collective-permute-done | bytes 524320 | tf_op jit(solution)/shard_map/ppermute | solution.py:64
  440.2 3.3 collective-permute-start.15
  443.5 7.0 %collective-permute-done.14 = bf16[32,4096]{1,0:T(8,128)(2,1)S(1)} collective-permute-done((bf16[32,4096]{1,0:T(8,128)(2,1)S(1)}, bf16[32,4096]{1,0:T(8,128)(2,1)S(1)}, u32[]{:S(2)}, u32[]{:S(2)}) %collective-permute-start.14) | collective-permute-done | bytes 262176 | tf_op jit(solution)/shard_map/ppermute | solution.py:66
  450.8 2.0 copy-done.5
  452.8 1.9 collective-permute-start.28
  458.5 6.5 %collective-permute-done.29 = bf16[64,4096]{1,0:T(8,128)(2,1)S(1)} collective-permute-done((bf16[64,4096]{1,0:T(8,128)(2,1)S(1)}, bf16[64,4096]{1,0:T(8,128)(2,1)S(1)}, u32[]{:S(2)}, u32[]{:S(2)}) %collective-permute-start.29) | collective-permute-done | bytes 524320 | tf_op jit(solution)/shard_map/ppermute | solution.py:64
  465.2 3.3 collective-permute-start.31
  469.3 3.4 collective-permute-done.30
  (150 shorter events, 44.1 us)
Async XLA Ops:
  0.6 4.3 copy-start.2
  37.7 2.0 copy-start
  40.8 69.5 %collective-permute-start = (f32[64,4096]{1,0:T(8,128)}, f32[64,4096]{1,0:T(8,128)S(1)}, u32[]{:S(2)}, u32[]{:S(2)}) collective-permute-start(f32[64,4096]{1,0:T(8,128)} %pad_maximum_fusion), channel_id=1, source_target_pairs={{0,8},{8,16},{16,24},{24,0},{1,9},{9,17},{17,25},{25,1},{2,10},{10... | collective-permute-start | bytes 3145736 | tf_op jit(solution)/shard_map/ppermute | solution.py:52
  47.7 3.4 slice-start
  47.7 4.7 slice-start.1
  55.0 2.0 copy-start.1
  57.0 3.3 copy-start.6
  57.0 7.7 %copy-start.9 = (bf16[1,2,4096]{2,1,0:T(2,128)(2,1)S(1)}, bf16[1,2,4096]{2,1,0:T(2,128)(2,1)}, u32[]{:S(2)}) copy-start(bf16[1,2,4096]{2,1,0:T(2,128)(2,1)} %param.31) | copy-start | bytes 49156
  57.0 7.8 %copy-start.7 = (bf16[8,4096]{1,0:T(8,128)(2,1)S(1)}, bf16[8,4096]{1,0:T(8,128)(2,1)}, u32[]{:S(2)}) copy-start(bf16[8,4096]{1,0:T(8,128)(2,1)} %param.18) | copy-start | bytes 196612
  58.2 57.2 %collective-permute-start.16 = (f32[64,4096]{1,0:T(8,128)}, f32[64,4096]{1,0:T(8,128)S(1)}, u32[]{:S(2)}, u32[]{:S(2)}) collective-permute-start(f32[64,4096]{1,0:T(8,128)} %pad_maximum_fusion.4), channel_id=1, source_target_pairs={{0,8},{8,16},{16,24},{24,0},{1,9},{9,17},{17,25},{25,1},{2,10},{10... | collective-permute-start | bytes 3145736 | tf_op jit(solution)/shard_map/ppermute | solution.py:52
  61.5 394.0 %collective-permute-start.32 = (bf16[2,512,128]{2,1,0:T(8,128)(2,1)}, bf16[2,512,128]{2,1,0:T(8,128)(2,1)}, u32[]{:S(2)}, u32[]{:S(2)}) collective-permute-start(bf16[2,512,128]{2,1,0:T(8,128)(2,1)} %fusion.139), channel_id=1, source_target_pairs={{0,4},{1,5},{2,6},{3,7},{4,0},{5,1},{6,2},{7,3},{8,20},{9,21},{10,... | collective-permute-start | bytes 786440 | tf_op jit(solution)/shard_map/ppermute | solution.py:113
  65.0 8.1 %copy-start.10 = (s32[8]{0:T(128)S(1)}, s32[8]{0:T(128)}, u32[]{:S(2)}) copy-start(s32[8]{0:T(128)} %len_ref.1) | copy-start | bytes 100
  112.9 37.0 %collective-permute-start.2 = (f32[64,4096]{1,0:T(8,128)}, f32[64,4096]{1,0:T(8,128)}, u32[]{:S(2)}, u32[]{:S(2)}) collective-permute-start(f32[64,4096]{1,0:T(8,128)} %pad_maximum_fusion.1), channel_id=1, source_target_pairs={{0,24},{8,0},{16,8},{24,16},{1,25},{9,1},{17,9},{25,17},{2,26},{10... | collective-permute-start | bytes 3145736 | tf_op jit(solution)/shard_map/ppermute | solution.py:53
  114.9 35.0 %collective-permute-start.1 = (f32[32,4096]{1,0:T(8,128)S(1)}, f32[32,4096]{1,0:T(8,128)}, u32[]{:S(2)}, u32[]{:S(2)}) collective-permute-start(f32[32,4096]{1,0:T(8,128)S(1)} %get-tuple-element.67), channel_id=1, source_target_pairs={{0,8},{8,16},{16,24},{24,0},{1,9},{9,17},{17,25},{25,1},{2,10},{10... | collective-permute-start | bytes 1572872 | tf_op jit(solution)/shard_map/ppermute | solution.py:54
  118.7 43.1 %collective-permute-start.18 = (f32[64,4096]{1,0:T(8,128)}, f32[64,4096]{1,0:T(8,128)}, u32[]{:S(2)}, u32[]{:S(2)}) collective-permute-start(f32[64,4096]{1,0:T(8,128)} %pad_maximum_fusion.5), channel_id=1, source_target_pairs={{0,24},{8,0},{16,8},{24,16},{1,25},{9,1},{17,9},{25,17},{2,26},{10... | collective-permute-start | bytes 3145736 | tf_op jit(solution)/shard_map/ppermute | solution.py:53
  149.8 10.5 %collective-permute-start.17 = (f32[32,4096]{1,0:T(8,128)}, f32[32,4096]{1,0:T(8,128)S(1)}, u32[]{:S(2)}, u32[]{:S(2)}) collective-permute-start(f32[32,4096]{1,0:T(8,128)} %get-tuple-element.57), channel_id=1, source_target_pairs={{0,8},{8,16},{16,24},{24,0},{1,9},{9,17},{17,25},{25,1},{2,10},{10... | collective-permute-start | bytes 1572872 | tf_op jit(solution)/shard_map/ppermute | solution.py:54
  151.7 21.4 %collective-permute-start.3 = (f32[32,4096]{1,0:T(8,128)S(1)}, f32[32,4096]{1,0:T(8,128)S(1)}, u32[]{:S(2)}, u32[]{:S(2)}) collective-permute-start(f32[32,4096]{1,0:T(8,128)S(1)} %get-tuple-element.49), channel_id=1, source_target_pairs={{0,24},{8,0},{16,8},{24,16},{1,25},{9,1},{17,9},{25,17},{2,26},{10... | collective-permute-start | bytes 1572872 | tf_op jit(solution)/shard_map/ppermute | solution.py:55
  163.5 16.3 %collective-permute-start.19 = (f32[32,4096]{1,0:T(8,128)S(1)}, f32[32,4096]{1,0:T(8,128)S(1)}, u32[]{:S(2)}, u32[]{:S(2)}) collective-permute-start(f32[32,4096]{1,0:T(8,128)S(1)} %get-tuple-element.45), channel_id=1, source_target_pairs={{0,24},{8,0},{16,8},{24,16},{1,25},{9,1},{17,9},{25,17},{2,26},{10... | collective-permute-start | bytes 1572872 | tf_op jit(solution)/shard_map/ppermute | solution.py:55
  184.1 17.4 %collective-permute-start.20 = (bf16[64,4096]{1,0:T(8,128)(2,1)}, bf16[64,4096]{1,0:T(8,128)(2,1)S(1)}, u32[]{:S(2)}, u32[]{:S(2)}) collective-permute-start(bf16[64,4096]{1,0:T(8,128)(2,1)} %get-tuple-element.33), channel_id=1, source_target_pairs={{0,24},{8,0},{16,8},{24,16},{1,25},{9,1},{17,9},{25,17},{2,26},{10... | collective-permute-start | bytes 1572872 | tf_op jit(solution)/shard_map/ppermute | solution.py:65
  185.8 15.7 %collective-permute-start.21 = (bf16[64,4096]{1,0:T(8,128)(2,1)}, bf16[64,4096]{1,0:T(8,128)(2,1)S(1)}, u32[]{:S(2)}, u32[]{:S(2)}) collective-permute-start(bf16[64,4096]{1,0:T(8,128)(2,1)} %get-tuple-element.33), channel_id=1, source_target_pairs={{0,8},{8,16},{16,24},{24,0},{1,9},{9,17},{17,25},{25,1},{2,10},{10... | collective-permute-start | bytes 1572872 | tf_op jit(solution)/shard_map/ppermute | solution.py:64
  186.2 31.4 %collective-permute-start.5 = (bf16[64,4096]{1,0:T(8,128)(2,1)}, bf16[64,4096]{1,0:T(8,128)(2,1)S(1)}, u32[]{:S(2)}, u32[]{:S(2)}) collective-permute-start(bf16[64,4096]{1,0:T(8,128)(2,1)} %get-tuple-element.93), channel_id=1, source_target_pairs={{0,8},{8,16},{16,24},{24,0},{1,9},{9,17},{17,25},{25,1},{2,10},{10... | collective-permute-start | bytes 1572872 | tf_op jit(solution)/shard_map/ppermute | solution.py:64
  197.5 20.9 %collective-permute-start.4 = (bf16[64,4096]{1,0:T(8,128)(2,1)}, bf16[64,4096]{1,0:T(8,128)(2,1)S(1)}, u32[]{:S(2)}, u32[]{:S(2)}) collective-permute-start(bf16[64,4096]{1,0:T(8,128)(2,1)} %get-tuple-element.93), channel_id=1, source_target_pairs={{0,24},{8,0},{16,8},{24,16},{1,25},{9,1},{17,9},{25,17},{2,26},{10... | collective-permute-start | bytes 1572872 | tf_op jit(solution)/shard_map/ppermute | solution.py:65
  201.5 253.9 %collective-permute-start.33 = (bf16[2,512,128]{2,1,0:T(8,128)(2,1)}, bf16[2,512,128]{2,1,0:T(8,128)(2,1)}, u32[]{:S(2)}, u32[]{:S(2)}) collective-permute-start(bf16[2,512,128]{2,1,0:T(8,128)(2,1)} %fusion.133), channel_id=1, source_target_pairs={{0,12},{1,13},{2,14},{3,15},{4,8},{5,9},{6,10},{7,11},{8,28},{9,29... | collective-permute-start | bytes 786440 | tf_op jit(solution)/shard_map/ppermute | solution.py:113
  201.6 19.7 %collective-permute-start.22 = (bf16[32,4096]{1,0:T(8,128)(2,1)S(1)}, bf16[32,4096]{1,0:T(8,128)(2,1)S(1)}, u32[]{:S(2)}, u32[]{:S(2)}) collective-permute-start(bf16[32,4096]{1,0:T(8,128)(2,1)S(1)} %slice.467), channel_id=1, source_target_pairs={{0,8},{8,16},{16,24},{24,0},{1,9},{9,17},{17,25},{25,1},{2,10},{10... | collective-permute-start | bytes 786440 | tf_op jit(solution)/shard_map/ppermute | solution.py:66
  217.6 6.4 %collective-permute-start.23 = (bf16[32,4096]{1,0:T(8,128)(2,1)S(1)}, bf16[32,4096]{1,0:T(8,128)(2,1)S(1)}, u32[]{:S(2)}, u32[]{:S(2)}) collective-permute-start(bf16[32,4096]{1,0:T(8,128)(2,1)S(1)} %slice.468), channel_id=1, source_target_pairs={{0,24},{8,0},{16,8},{24,16},{1,25},{9,1},{17,9},{25,17},{2,26},{10... | collective-permute-start | bytes 786440 | tf_op jit(solution)/shard_map/ppermute | solution.py:67
  218.4 42.7 %collective-permute-start.6 = (bf16[32,4096]{1,0:T(8,128)(2,1)S(1)}, bf16[32,4096]{1,0:T(8,128)(2,1)S(1)}, u32[]{:S(2)}, u32[]{:S(2)}) collective-permute-start(bf16[32,4096]{1,0:T(8,128)(2,1)S(1)} %slice.436), channel_id=1, source_target_pairs={{0,8},{8,16},{16,24},{24,0},{1,9},{9,17},{17,25},{25,1},{2,10},{10... | collective-permute-start | bytes 786440 | tf_op jit(solution)/shard_map/ppermute | solution.py:66
  221.3 39.9 %collective-permute-start.7 = (bf16[32,4096]{1,0:T(8,128)(2,1)S(1)}, bf16[32,4096]{1,0:T(8,128)(2,1)S(1)}, u32[]{:S(2)}, u32[]{:S(2)}) collective-permute-start(bf16[32,4096]{1,0:T(8,128)(2,1)S(1)} %slice.437), channel_id=1, source_target_pairs={{0,24},{8,0},{16,8},{24,16},{1,25},{9,1},{17,9},{25,17},{2,26},{10... | collective-permute-start | bytes 786440 | tf_op jit(solution)/shard_map/ppermute | solution.py:67
  225.5 35.7 %copy-start.8 = (bf16[256,4096]{1,0:T(8,128)(2,1)S(1)}, bf16[256,4096]{1,0:T(8,128)(2,1)}, u32[]{:S(2)}) copy-start(bf16[256,4096]{1,0:T(8,128)(2,1)} %constant_dynamic-update-slice_fusion.3) | copy-start | bytes 6291460
  311.2 63.0 %copy-start.3 = (f32[256,4096]{1,0:T(8,128)}, f32[256,4096]{1,0:T(8,128)S(1)}, u32[]{:S(2)}) copy-start(f32[256,4096]{1,0:T(8,128)S(1)} %fusion.11) | copy-start | bytes 12582916
  327.6 27.5 %copy-start.4 = (f32[256,4096]{1,0:T(8,128)}, f32[256,4096]{1,0:T(8,128)S(1)}, u32[]{:S(2)}) copy-start(f32[256,4096]{1,0:T(8,128)S(1)} %fusion.13) | copy-start | bytes 12582916
  327.8 27.3 %collective-permute-start.8 = (f32[64,4096]{1,0:T(8,128)S(1)}, f32[64,4096]{1,0:T(8,128)S(1)}, u32[]{:S(2)}, u32[]{:S(2)}) collective-permute-start(f32[64,4096]{1,0:T(8,128)S(1)} %pad_maximum_fusion.2), channel_id=1, source_target_pairs={{0,8},{8,16},{16,24},{24,0},{1,9},{9,17},{17,25},{25,1},{2,10},{10... | collective-permute-start | bytes 3145736 | tf_op jit(solution)/shard_map/ppermute | solution.py:52
  328.3 45.9 %collective-permute-start.24 = (f32[64,4096]{1,0:T(8,128)S(1)}, f32[64,4096]{1,0:T(8,128)S(1)}, u32[]{:S(2)}, u32[]{:S(2)}) collective-permute-start(f32[64,4096]{1,0:T(8,128)S(1)} %pad_maximum_fusion.6), channel_id=1, source_target_pairs={{0,8},{8,16},{16,24},{24,0},{1,9},{9,17},{17,25},{25,1},{2,10},{10... | collective-permute-start | bytes 3145736 | tf_op jit(solution)/shard_map/ppermute | solution.py:52
  357.1 49.5 %collective-permute-start.10 = (f32[64,4096]{1,0:T(8,128)}, f32[64,4096]{1,0:T(8,128)}, u32[]{:S(2)}, u32[]{:S(2)}) collective-permute-start(f32[64,4096]{1,0:T(8,128)} %pad_maximum_fusion.3), channel_id=1, source_target_pairs={{0,24},{8,0},{16,8},{24,16},{1,25},{9,1},{17,9},{25,17},{2,26},{10... | collective-permute-start | bytes 3145736 | tf_op jit(solution)/shard_map/ppermute | solution.py:53
  357.1 49.3 %collective-permute-start.9 = (f32[32,4096]{1,0:T(8,128)}, f32[32,4096]{1,0:T(8,128)}, u32[]{:S(2)}, u32[]{:S(2)}) collective-permute-start(f32[32,4096]{1,0:T(8,128)} %get-tuple-element.62), channel_id=1, source_target_pairs={{0,8},{8,16},{16,24},{24,0},{1,9},{9,17},{17,25},{25,1},{2,10},{10... | collective-permute-start | bytes 1572872 | tf_op jit(solution)/shard_map/ppermute | solution.py:54
  376.2 43.4 %collective-permute-start.26 = (f32[64,4096]{1,0:T(8,128)}, f32[64,4096]{1,0:T(8,128)}, u32[]{:S(2)}, u32[]{:S(2)}) collective-permute-start(f32[64,4096]{1,0:T(8,128)} %pad_maximum_fusion.7), channel_id=1, source_target_pairs={{0,24},{8,0},{16,8},{24,16},{1,25},{9,1},{17,9},{25,17},{2,26},{10... | collective-permute-start | bytes 3145736 | tf_op jit(solution)/shard_map/ppermute | solution.py:53
  406.5 13.2 %collective-permute-start.25 = (f32[32,4096]{1,0:T(8,128)}, f32[32,4096]{1,0:T(8,128)S(1)}, u32[]{:S(2)}, u32[]{:S(2)}) collective-permute-start(f32[32,4096]{1,0:T(8,128)} %get-tuple-element.50), channel_id=1, source_target_pairs={{0,8},{8,16},{16,24},{24,0},{1,9},{9,17},{17,25},{25,1},{2,10},{10... | collective-permute-start | bytes 1572872 | tf_op jit(solution)/shard_map/ppermute | solution.py:54
  408.4 15.6 %collective-permute-start.11 = (f32[32,4096]{1,0:T(8,128)S(1)}, f32[32,4096]{1,0:T(8,128)S(1)}, u32[]{:S(2)}, u32[]{:S(2)}) collective-permute-start(f32[32,4096]{1,0:T(8,128)S(1)} %get-tuple-element.47), channel_id=1, source_target_pairs={{0,24},{8,0},{16,8},{24,16},{1,25},{9,1},{17,9},{25,17},{2,26},{10... | collective-permute-start | bytes 1572872 | tf_op jit(solution)/shard_map/ppermute | solution.py:55
  421.3 12.1 %collective-permute-start.27 = (f32[32,4096]{1,0:T(8,128)S(1)}, f32[32,4096]{1,0:T(8,128)S(1)}, u32[]{:S(2)}, u32[]{:S(2)}) collective-permute-start(f32[32,4096]{1,0:T(8,128)S(1)} %get-tuple-element.43), channel_id=1, source_target_pairs={{0,24},{8,0},{16,8},{24,16},{1,25},{9,1},{17,9},{25,17},{2,26},{10... | collective-permute-start | bytes 1572872 | tf_op jit(solution)/shard_map/ppermute | solution.py:55
  425.8 14.3 %collective-permute-start.12 = (bf16[64,4096]{1,0:T(8,128)(2,1)S(1)}, bf16[64,4096]{1,0:T(8,128)(2,1)S(1)}, u32[]{:S(2)}, u32[]{:S(2)}) collective-permute-start(bf16[64,4096]{1,0:T(8,128)(2,1)S(1)} %get-tuple-element.37), channel_id=1, source_target_pairs={{0,24},{8,0},{16,8},{24,16},{1,25},{9,1},{17,9},{25,17},{2,26},{10... | collective-permute-start | bytes 1572872 | tf_op jit(solution)/shard_map/ppermute | solution.py:65
  429.6 10.4 %collective-permute-start.13 = (bf16[64,4096]{1,0:T(8,128)(2,1)S(1)}, bf16[64,4096]{1,0:T(8,128)(2,1)S(1)}, u32[]{:S(2)}, u32[]{:S(2)}) collective-permute-start(bf16[64,4096]{1,0:T(8,128)(2,1)S(1)} %get-tuple-element.37), channel_id=1, source_target_pairs={{0,8},{8,16},{16,24},{24,0},{1,9},{9,17},{17,25},{25,1},{2,10},{10... | collective-permute-start | bytes 1572872 | tf_op jit(solution)/shard_map/ppermute | solution.py:64
  440.0 10.5 %collective-permute-start.14 = (bf16[32,4096]{1,0:T(8,128)(2,1)S(1)}, bf16[32,4096]{1,0:T(8,128)(2,1)S(1)}, u32[]{:S(2)}, u32[]{:S(2)}) collective-permute-start(bf16[32,4096]{1,0:T(8,128)(2,1)S(1)} %slice.452), channel_id=1, source_target_pairs={{0,8},{8,16},{16,24},{24,0},{1,9},{9,17},{17,25},{25,1},{2,10},{10... | collective-permute-start | bytes 786440 | tf_op jit(solution)/shard_map/ppermute | solution.py:66
  440.2 10.3 %collective-permute-start.15 = (bf16[32,4096]{1,0:T(8,128)(2,1)S(1)}, bf16[32,4096]{1,0:T(8,128)(2,1)S(1)}, u32[]{:S(2)}, u32[]{:S(2)}) collective-permute-start(bf16[32,4096]{1,0:T(8,128)(2,1)S(1)} %slice.453), channel_id=1, source_target_pairs={{0,24},{8,0},{16,8},{24,16},{1,25},{9,1},{17,9},{25,17},{2,26},{10... | collective-permute-start | bytes 786440 | tf_op jit(solution)/shard_map/ppermute | solution.py:67
  450.8 2.0 copy-start.5
  452.8 12.4 %collective-permute-start.28 = (bf16[64,4096]{1,0:T(8,128)(2,1)S(1)}, bf16[64,4096]{1,0:T(8,128)(2,1)S(1)}, u32[]{:S(2)}, u32[]{:S(2)}) collective-permute-start(bf16[64,4096]{1,0:T(8,128)(2,1)S(1)} %get-tuple-element.31), channel_id=1, source_target_pairs={{0,24},{8,0},{16,8},{24,16},{1,25},{9,1},{17,9},{25,17},{2,26},{10... | collective-permute-start | bytes 1572872 | tf_op jit(solution)/shard_map/ppermute | solution.py:65
  454.7 10.4 %collective-permute-start.29 = (bf16[64,4096]{1,0:T(8,128)(2,1)S(1)}, bf16[64,4096]{1,0:T(8,128)(2,1)S(1)}, u32[]{:S(2)}, u32[]{:S(2)}) collective-permute-start(bf16[64,4096]{1,0:T(8,128)(2,1)S(1)} %get-tuple-element.31), channel_id=1, source_target_pairs={{0,8},{8,16},{16,24},{24,0},{1,9},{9,17},{17,25},{25,1},{2,10},{10... | collective-permute-start | bytes 1572872 | tf_op jit(solution)/shard_map/ppermute | solution.py:64
  465.1 7.7 %collective-permute-start.30 = (bf16[32,4096]{1,0:T(8,128)(2,1)S(1)}, bf16[32,4096]{1,0:T(8,128)(2,1)S(1)}, u32[]{:S(2)}, u32[]{:S(2)}) collective-permute-start(bf16[32,4096]{1,0:T(8,128)(2,1)S(1)} %slice.483), channel_id=1, source_target_pairs={{0,8},{8,16},{16,24},{24,0},{1,9},{9,17},{17,25},{25,1},{2,10},{10... | collective-permute-start | bytes 786440 | tf_op jit(solution)/shard_map/ppermute | solution.py:66
  465.2 7.5 %collective-permute-start.31 = (bf16[32,4096]{1,0:T(8,128)(2,1)S(1)}, bf16[32,4096]{1,0:T(8,128)(2,1)S(1)}, u32[]{:S(2)}, u32[]{:S(2)}) collective-permute-start(bf16[32,4096]{1,0:T(8,128)(2,1)S(1)} %slice.484), channel_id=1, source_target_pairs={{0,24},{8,0},{16,8},{24,16},{1,25},{9,1},{17,9},{25,17},{2,26},{10... | collective-permute-start | bytes 786440 | tf_op jit(solution)/shard_map/ppermute | solution.py:67

commit v2 on v1

--- a/solution.py
+++ b/solution.py
@@ -38,34 +38,301 @@
     return (jax.nn.silu(upgate[:, 1].astype(F32)) * upgate[:, 0].astype(F32)).astype(BF16)
 
 
-def ring_maps(tp_size):
-    fwd = [(i, (i + 1) % tp_size) for i in range(tp_size)]
-    bwd = [(i, (i - 1) % tp_size) for i in range(tp_size)]
-    return fwd, bwd
-
-
-def ring_reduce_scatter(part, tp_size):
-    fwd, bwd = ring_maps(tp_size)
-    rows = part.shape[0] // tp_size
-    half = rows // 2
-    blk = [part[j * rows:(j + 1) * rows] for j in range(tp_size)]
-    got_f = lax.ppermute(jnp.concatenate([blk[2][:half], blk[1][half:]]), 'tp', fwd)
-    got_b = lax.ppermute(jnp.concatenate([blk[3][:half], blk[2][half:]]), 'tp', bwd)
-    last_f = lax.ppermute(blk[1][:half] + got_f[:half], 'tp', fwd)
-    last_b = lax.ppermute(blk[3][half:] + got_b[half:], 'tp', bwd)
-    top = blk[0][:half] + (last_f + got_b[:half])
-    bot = blk[0][half:] + (got_f[half:] + last_b)
-    return jnp.concatenate([top, bot])
-
-
-def ring_all_gather(own, tp_size):
-    fwd, bwd = ring_maps(tp_size)
-    half = own.shape[0] // 2
-    prev_blk = lax.ppermute(own, 'tp', fwd)
-    next_blk = lax.ppermute(own, 'tp', bwd)
-    far_top = lax.ppermute(prev_blk[:half], 'tp', fwd)
-    far_bot = lax.ppermute(next_blk[half:], 'tp', bwd)
-    return [own, next_blk, jnp.concatenate([far_top, far_bot]), prev_blk]
+MESH = pl.DeviceIdType.MESH
+SUB = 512
+
+
+def mega_kernel(attn, xown, gain, wo_hbm, wug_hbm, wd_hbm, out_hbm, dense_hbm,
+                part, r1, r2, nfull, hown, act, wbuf, dbuf, raw, f32s,
+                s1_send, s1_recv, s2_send, s2_recv, ag_send, ag_recv,
+                w_sem, d_sem, raw_sem, put_sem, out_sem):
+    tp_size = lax.axis_size('tp')
+    me = lax.axis_index('tp')
+    right, left = lax.rem(me + 1, tp_size), lax.rem(me + tp_size - 1, tp_size)
+    _, n_grp, rows, width = part.shape
+    blk = rows // tp_size
+    half = blk // 2
+    depth = wug_hbm.shape[0]
+    n_tile = dense_hbm.shape[0]
+    n_up = n_tile // 2
+    n_down = wd_hbm.shape[1] // SUB
+    k_out = wo_hbm.shape[0]
+    peers = (right, left)
+
+    barrier = pltpu.get_barrier_semaphore()
+    for peer in peers:
+        pl.semaphore_signal(barrier, inc=1, device_id={'tp': peer}, device_id_type=MESH)
+    pl.semaphore_wait(barrier, 2)
+
+    def remote(src, dst, send, recv, way):
+        return pltpu.make_async_remote_copy(src_ref=src, dst_ref=dst, send_sem=send, recv_sem=recv,
+                                            device_id={'tp': peers[way]}, device_id_type=MESH)
+
+    def s1_copy(st, h, g, way):
+        src = part.at[h, g, pl.ds(blk + half + way * blk, blk)]
+        return remote(src, r1.at[st, h, way, g], s1_send.at[st, h, way, g], s1_recv.at[st, h, way, g], way)
+
+    def s2_copy(st, h, g, way):
+        src = part.at[h, g, pl.ds(blk if way == 0 else 3 * blk + half, half)]
+        return remote(src, r2.at[st, h, way, g], s2_send.at[st, h, way, g], s2_recv.at[st, h, way, g], way)
+
+    def ag1_copy(st, h, way):
+        return remote(nfull.at[h, pl.ds(0, blk)], nfull.at[h, pl.ds(3 * blk if way == 0 else blk, blk)],
+                      ag_send.at[st, h, way, 0], ag_recv.at[st, h, way, 0], way)
+
+    def ag2_copy(st, h, way):
+        src = nfull.at[h, pl.ds(3 * blk if way == 0 else blk + half, half)]
+        return remote(src, nfull.at[h, pl.ds(2 * blk + way * half, half)],
+                      ag_send.at[st, h, way, 1], ag_recv.at[st, h, way, 1], way)
+
+    def send_s1(st, h, g):
+        for way in range(2):
+            s1_copy(st, h, g, way).start()
+
+    def ev_s2(st, h, g):
+        for way in range(2):
+            s1_copy(st, h, g, way).wait_recv()
+        part[h, g, blk:blk + half] += r1[st, h, 0, g, half:]
+        s2_copy(st, h, g, 0).start()
+        part[h, g, 3 * blk + half:] += r1[st, h, 1, g, :half]
+        s2_copy(st, h, g, 1).start()
+
+    def ev_final(st, h):
+        for g in range(n_grp):
+            for way in range(2):
+                s2_copy(st, h, g, way).wait_recv()
+            cols = slice(g * width, (g + 1) * width)
+            base = xown if st == 0 else hown
+            top = part[h, g, :half] + (r1[st, h, 1, g, half:] + r2[st, h, 0, g])
+            bot = part[h, g, half:blk] + (r1[st, h, 0, g, :half] + r2[st, h, 1, g])
+            total = jnp.concatenate([top, bot], axis=0).astype(BF16)
+            new = (base[h, :, cols].astype(F32) + total.astype(F32)).astype(BF16)
+            if st == 0:
+                hown[h, :, cols] = new
+            else:
+                nfull[h, :blk, cols] = new
+        if st == 0:
+            for r in range(0, blk, 16):
+                val = hown[h, r:r + 16].astype(F32)
+                inv = lax.rsqrt(jnp.mean(val * val, axis=-1, keepdims=True) + NORM_EPS)
+                nfull[h, r:r + 16] = (val * inv * gain[...].astype(F32)).astype(BF16)
+        for way in range(2):
+            ag1_copy(st, h, way).start()
+
+    def ev_ag2(st, h):
+        for way in range(2):
+            ag1_copy(st, h, way).wait_recv()
+            ag2_copy(st, h, way).start()
+
+    def ev_ag_done(st, h):
+        for way in range(2):
+            ag2_copy(st, h, way).wait_recv()
+
+    def drain(st, h):
+        for way in range(2):
+            for g in range(n_grp):
+                s1_copy(st, h, g, way).wait_send()
+                s2_copy(st, h, g, way).wait_send()
+            ag1_copy(st, h, way).wait_send()
+            ag2_copy(st, h, way).wait_send()
+
+    def wo_load(c, slot):
+        return pltpu.make_async_copy(wo_hbm.at[:, pl.ds(pl.multiple_of(c * SUB, SUB), SUB)], dbuf.at[slot, pl.ds(0, k_out)], d_sem.at[slot])
+
+    def wd_load(c, slot):
+        return pltpu.make_async_copy(wd_hbm.at[:, pl.ds(pl.multiple_of(c * SUB, SUB), SUB)], dbuf.at[slot], d_sem.at[slot])
+
+    def raw_load(i, slot):
+        return pltpu.make_async_copy(wug_hbm.at[:, :, pl.ds(pl.multiple_of(i * 128, 128), 128)], raw.at[slot], raw_sem.at[slot])
+
+    def put_store(i, slot):
+        return pltpu.make_async_copy(wbuf.at[slot, 0], dense_hbm.at[i], put_sem.at[slot])
+
+    def up_load(c, slot):
+        return pltpu.make_async_copy(dense_hbm.at[pl.ds(2 * c, 2)], wbuf.at[slot], w_sem.at[slot])
+
+    def split_tiles(lo, hi):
+        step = 4 * 256
+        flat = raw.reshape(2, 2 * depth, 128)
+
+        @pl.loop(lo, hi)
+        def _(i):
+            slot = lax.rem(i, 2)
+            raw_load(i, slot).wait()
+
+            @pl.when(i >= 2)
+            def _():
+                put_store(i - 2, slot).wait()
+
+            @pl.loop(0, 2 * depth // step)
+            def _(p):
+                for q in range(4):
+                    f32s[q] = flat[slot, pl.ds(pl.multiple_of(p * step + q * 256, 256), 256)].astype(F32)
+                for q in range(4):
+                    dst = pl.ds(pl.multiple_of(p * (step // 2) + q * 128, 128), 128)
+                    for k in range(2):
+                        wbuf[slot, 0, k, dst] = f32s[q, pl.ds(k, 128, stride=2)].astype(BF16)
+
+            @pl.when(i + 2 < n_tile)
+            def _():
+                raw_load(i + 2, slot).start()
+            put_store(i, slot).start()
+
+    def up_chunks(h, lo, hi):
+        @pl.loop(lo, hi)
+        def _(c):
+            slot = lax.rem(c, 2)
+            up_load(c, slot).wait()
+            res = []
+            for k in range(2):
+                w = jnp.concatenate([wbuf[slot, 0, k], wbuf[slot, 1, k]], axis=-1)
+                res.append(jnp.dot(nfull[h], w, preferred_element_type=F32).astype(BF16).astype(F32))
+            act[:, pl.ds(pl.multiple_of(c * 256, 256), 256)] = (jax.nn.silu(res[1]) * res[0]).astype(BF16)
+
+            @pl.when(c + 2 < n_up)
+            def _():
+                up_load(c + 2, slot).start()
+
+    def down_group(h, g):
+        for q in range(2):
+            c = 2 * g + q
+            wd_load(c, q).wait()
+            part[h, g, :, q * SUB:(q + 1) * SUB] = jnp.dot(act[...], dbuf[q], preferred_element_type=F32)
+
+            @pl.when(c + 2 < n_down)
+            def _():
+                wd_load(c + 2, q).start()
+        send_s1(1, h, g)
+
+    def write_out(h):
+        for j in range(tp_size):
+            row = h * rows + lax.rem(me + j, tp_size) * blk
+            yield pltpu.make_async_copy(nfull.at[h, pl.ds(j * blk, blk)], out_hbm.at[pl.ds(pl.multiple_of(row, blk), blk)], out_sem.at[h, j])
+
+    for slot in range(2):
+        wo_load(slot, slot).start()
+        raw_load(slot, slot).start()
+
+    @pl.loop(0, n_grp)
+    def _(g):
+        for q in range(2):
+            c = 2 * g + q
+            wo_load(c, q).wait()
+            for h in range(2):
+                part[h, g, :, q * SUB:(q + 1) * SUB] = jnp.dot(attn[h], dbuf[q, :k_out], preferred_element_type=F32)
+
+            @pl.when(c + 2 < n_down)
+            def _():
+                wo_load(c + 2, q).start()
+        send_s1(0, 0, g)
+
+    for q in range(2):
+        wd_load(q, q).start()
+    cut = [3, 6, 9, 12, 18, 25, 28]
+    done = 0
+    for g in range(n_grp):
+        split_tiles(done, cut[g])
+        done = cut[g]
+        ev_s2(0, 0, g)
+    send_s1(0, 1, 0)
+    split_tiles(done, cut[4])
+    ev_final(0, 0)
+    send_s1(0, 1, 1)
+    split_tiles(cut[4], cut[5])
+    ev_ag2(0, 0)
+    send_s1(0, 1, 2)
+    send_s1(0, 1, 3)
+    split_tiles(cut[5], n_tile)
+    for i in (n_tile - 2, n_tile - 1):
+        put_store(i, i % 2).wait()
+    for slot in range(2):
+        up_load(slot, slot).start()
+    ev_s2(0, 1, 0)
+    ev_ag_done(0, 0)
+    up_chunks(0, 0, 3)
+    ev_s2(0, 1, 1)
+    up_chunks(0, 3, 7)
+    ev_s2(0, 1, 2)
+    up_chunks(0, 7, 12)
+    ev_s2(0, 1, 3)
+    up_chunks(0, 12, n_up)
+    for slot in range(2):
+        up_load(slot, slot).start()
+    drain(0, 0)
+    down_group(0, 0)
+    down_group(0, 1)
+    ev_final(0, 1)
+    down_group(0, 2)
+    down_group(0, 3)
+    for q in range(2):
+        wd_load(q, q).start()
+    ev_s2(1, 0, 0)
+    ev_ag2(0, 1)
+    ev_s2(1, 0, 1)
+    ev_ag_done(0, 1)
+    up_chunks(1, 0, 2)
+    ev_s2(1, 0, 2)
+    up_chunks(1, 2, 6)
+    ev_s2(1, 0, 3)
+    up_chunks(1, 6, n_up)
+    drain(0, 1)
+    ev_final(1, 0)
+    down_group(1, 0)
+    down_group(1, 1)
+    down_group(1, 2)
+    ev_ag2(1, 0)
+    down_group(1, 3)
+    for g in range(n_grp):
+        ev_s2(1, 1, g)
+    ev_ag_done(1, 0)
+    for copy in write_out(0):
+        copy.start()
+    ev_final(1, 1)
+    ev_ag2(1, 1)
+    ev_ag_done(1, 1)
+    for copy in write_out(1):
+        copy.start()
+    drain(1, 0)
+    drain(1, 1)
+    for h in range(2):
+        for copy in write_out(h):
+            copy.wait()
+
+
+def mega(attn, xown, gain, w_out, w_ug, w_down, tp_size):
+    halves, rows, k_out = attn.shape
+    depth, _, ffn = w_ug.shape
+    blk = rows // tp_size
+    n_grp = 4
+    width = depth // n_grp
+    vmem = pl.BlockSpec(memory_space=pltpu.VMEM)
+    hbm = pl.BlockSpec(memory_space=pl.ANY)
+    dma = pltpu.SemaphoreType.DMA
+    out, _ = pl.pallas_call(
+        mega_kernel,
+        in_specs=[vmem, vmem, vmem, hbm, hbm, hbm],
+        out_specs=[hbm, hbm],
+        out_shape=[jax.ShapeDtypeStruct((halves * rows, depth), BF16), jax.ShapeDtypeStruct((ffn // 128, 2, depth, 128), BF16)],
+        scratch_shapes=[
+            pltpu.VMEM((2, n_grp, rows, width), F32),
+            pltpu.VMEM((2, 2, 2, n_grp, blk, width), F32),
+            pltpu.VMEM((2, 2, 2, n_grp, blk // 2, width), F32),
+            pltpu.VMEM((2, rows, depth), BF16),
+            pltpu.VMEM((2, blk, depth), BF16),
+            pltpu.VMEM((rows, ffn), BF16),
+            pltpu.VMEM((2, 2, 2, depth, 128), BF16),
+            pltpu.VMEM((2, ffn, SUB), BF16),
+            pltpu.VMEM((2, depth, 2, 128), BF16),
+            pltpu.VMEM((4, 256, 128), F32),
+            dma((2, 2, 2, n_grp)), dma((2, 2, 2, n_grp)), dma((2, 2, 2, n_grp)), dma((2, 2, 2, n_grp)),
+            dma((2, 2, 2, 2)), dma((2, 2, 2, 2)),
+            dma((2,)), dma((2,)), dma((2,)), dma((2,)), dma((2, tp_size)),
+        ],
+        compiler_params=pltpu.CompilerParams(collective_id=0, has_side_effects=True, vmem_limit_bytes=62 * 2 ** 20),
+        cost_estimate=pl.CostEstimate(flops=6 * halves * rows * depth * ffn, bytes_accessed=4 * depth * ffn * 2, transcendentals=0),
+        name='prefill_tail',
+    )(attn, xown, gain, w_out, w_ug, w_down)
+    return out
 
 
 def roll_rows(vals, start):
@@ -184,21 +451,10 @@
         group = wo_a.shape[2] // head_dim
         w_out = wo_a[0].reshape(-1, wo_a.shape[3])
         attn, key_cache, val_cache = prompt_attention(x_prompt, s_len[0], wqkv_a[0], head_dim, group, norm_a[0, 0], half_len)
-        own_h, normed = [], []
-        for idx in range(2):
-            part = jnp.dot(roll_rows(attn[idx], t_idx * blk), w_out, preferred_element_type=F32)
-            own = lax.dynamic_slice_in_dim(x_prompt, idx * half_len + t_idx * blk, blk, axis=0)
-            own = residual(own, ring_reduce_scatter(part, tp_size))
-            own_h.append(own)
-            normed.append(jnp.concatenate(ring_all_gather(rms_norm(own, norm_a[0, 1]), tp_size)))
+        rolled = jnp.stack([roll_rows(part, t_idx * blk) for part in attn])
+        own = jnp.stack([lax.dynamic_slice_in_dim(x_prompt, idx * half_len + t_idx * blk, blk, axis=0) for idx in range(2)])
         k_prompt, v_prompt = hand_off(key_cache, val_cache, tp_size, side_size)
-        hidden = jnp.zeros_like(x_prompt)
-        for idx in range(2):
-            act = up_act(normed[idx], wug_a[0])
-            part = jnp.dot(act, wd_a[0], preferred_element_type=F32)
-            own = residual(own_h[idx], ring_reduce_scatter(part, tp_size))
-            for j, rows in enumerate(ring_all_gather(own, tp_size)):
-                hidden = lax.dynamic_update_slice_in_dim(hidden, rows, idx * half_len + lax.rem(t_idx + j, tp_size) * blk, axis=0)
+        hidden = mega(rolled, own, norm_a[0, 1:2], w_out, wug_a[0], wd_a[0], tp_size)
         kc = k_cache[0, :, :, :, 0]
         vc = v_cache[0, :, :, :, 0]
         y_out, k_new, v_new = decode_side(y_tok, c_len, kc, vc, wqkv_b[0, :, :, 0], wo_b[0, :, 0], wug_b[0], wd_b[0], norm_b[0])

time: 484 us -> 403 us (0.83)
  the two profiles are of different devices: /device:TPU:96 before, /device:TPU:100 now
where the time goes in v2:
time: 403 us; the launch traced here: 396 us
  Pallas kernels  238 us (59%)
  matrix products  81.5 us (20%)
  blocking collectives  34 us (8%)
  other arithmetic  18.3 us (5%)
  local copies, waits for them, and re-layouts  15.2 us (4%)
  starting transfers between devices  7.16 us (2%)
    pallas_call x1, Pallas kernels, mega(): pl.pallas_call(mega_kernel, in_specs=[vmem, vmem, vmem, hbm, hbm, hbm], o...  229 us
    dot_general x1, matrix products, up_act(): jnp.einsum('sd,dkf->skf', normed, w_ug, preferred_element_type=F32)  28.3 us
    psum x1, blocking collectives, decode_side(): lax.psum(jnp.einsum('bif,ifd->bd', attn_out.reshape(batch_rows, kv_loc, g...  17.7 us
    psum x1, blocking collectives, decode_side(): lax.psum(jnp.dot(act, w_down, preferred_element_type=F32), 'tp')  16.3 us
    dot_general x1, matrix products, decode_side(): jnp.dot(act, w_down, preferred_element_type=F32)  11.4 us
    unnamed x21, local copies, waits for them, and re-layouts  10.9 us
    dot_general x1, matrix products, prompt_attention(): jnp.einsum('sd,dhe->she', normed, w_qkv, preferred_element_type=F32)  10.7 us
    sub x2, matrix products, prompt_attention(): attn_prob = jax.nn.softmax(scores, axis=-1).astype(BF16)  8.58 us
  transfers between devices with their start and end apart: 2, of which 0 were waited for; matrix products, arithmetic and copies ran while one was open for 22% of the time, Pallas kernels for 60%

profile of v2, /device:TPU:100, one launch (start us, length us, event | category | flops | bytes accessed | tf_op | source)
XLA Modules:
  0.0 396.0 jit_solution(2137028515945361741)
XLA Ops:
  0.7 0.0 copy-start
  0.7 1.5 slice_bitcast_fusion.2
  2.2 3.1 fusion.11
  5.3 0.0 copy-done
  5.3 10.7 %fusion.40 = bf16[512,2,768]{2,0,1:T(8,128)(2,1)S(1)} fusion(bf16[4096,2,768]{2,1,0:T(2,128)(2,1)} %bitcast.173, bf16[512,4096]{1,0:T(8,128)(2,1)S(1)} %copy-done, f32[4096]{0:T(1024)S(1)} %bitcast.170, f32[512]{0:T(512)S(1)} %add_rsqrt_fusion), kind=kOutput, calls=%fused_computation.47 | convolution fusion | flops 6451625984 | bytes 18368512 | tf_op jit(solution)/shard_map/sd,dhe->she/dot_general | solution.py:347
  16.0 0.7 copy.81
  16.8 0.0 copy-start.4
  16.8 0.0 copy-start.3
  16.8 0.2 copy.120
  17.0 0.2 copy.123
  17.8 1.0 multiply_cosine_fusion
  18.8 0.2 fusion.66
  19.1 0.0 copy-start.1
  19.1 0.2 maximum_select_fusion
  19.3 0.8 fusion.83
  20.1 0.8 collective-permute-start
  20.9 0.7 fusion.77
  21.7 6.3 %collective-permute-start.1 = (bf16[2,512,128]{2,1,0:T(8,128)(2,1)}, bf16[2,512,128]{2,1,0:T(8,128)(2,1)}, u32[]{:S(2)}, u32[]{:S(2)}) collective-permute-start(bf16[2,512,128]{2,1,0:T(8,128)(2,1)} %fusion.77), channel_id=1, source_target_pairs={{0,12},{1,13},{2,14},{3,15},{4,8},{5,9},{6,10},{7,11},{8,28},{9,29... | collective-permute-start | bytes 786440 | tf_op jit(solution)/shard_map/ppermute | solution.py:380
  28.0 1.1 fusion.151
  29.0 0.0 copy-done.4
  29.1 0.1 fusion.89
  29.3 7.9 %fusion.56 = bf16[8,2,768]{2,0,1:T(8,128)(2,1)S(1)} fusion(bf16[4096,2,768]{2,1,0:T(2,128)(2,1)} %bitcast.156, bf16[8,4096]{1,0:T(8,128)(2,1)S(1)} %copy-done.3, f32[4096]{0:T(1024)S(1)} %bitcast.169, f32[8]{0:T(128)S(1)} %add_rsqrt_fusion.2), kind=kOutput, calls=%fused_computation.55 | convolution fusion | flops 100806656 | bytes 12689440 | tf_op jit(solution)/shard_map/bd,die->bie/dot_general | solution.py:417
  37.2 0.1 reshape.368
  37.3 0.1 fusion.152
  37.3 0.5 convert_element_type.198
  37.9 0.1 iota_compare_fusion.2
  38.0 1.5 copy.121
  39.5 2.4 copy.122
  41.9 0.8 fusion.76
  42.6 3.2 fusion.32
  45.9 5.0 %fusion.154 = (f32[2,4,256]{2,1,0:T(4,128)S(1)}, f32[2,4,256,512]{2,3,1,0:T(8,128)}) fusion(pred[256,512]{0,1:T(8,128)(4,1)} %fusion.76, bf16[512,2,64]{2,0,1:T(8,128)(2,1)} %copy-done.1, bf16[512,2,64]{2,0,1:T(8,128)(2,1)S(1)} %get-tuple-element.40, bf16[512,2,4,64]{3,0,2,1:T(8,128)(2,1)} %get-tuple-element.35, bf16[512,2,4,64]{3,0,2,1:T(8,128)(2,1)} %get-tuple-element.34), kind=kOutput, calls=%fused_computation.199 | convolution fusion | flops 274203136 | bytes 5644288 | tf_op jit(solution)/shard_map/sub | solution.py:359
  50.9 2.7 fusion.45
  53.6 0.2 copy.92
  53.9 0.1 fusion.84
  54.0 0.0 copy-done.2
  54.0 3.5 fusion.155
  57.5 1.9 convolution_convert_fusion
  59.4 0.2 copy.87
  59.7 0.0 copy-done.6
  59.7 0.1 multiply_cosine_fusion.1
  59.8 0.6 copy_bitcast_fusion
  60.4 0.1 fusion.132
  60.5 0.7 pad_maximum_fusion.5.kn_ref
  61.2 8.4 %cache_update.1 = (bf16[8,768,2,128]{3,2,1,0:T(2,128)(2,1)}, bf16[8,768,2,128]{3,2,1,0:T(2,128)(2,1)}) custom-call(s32[8]{0:T(128)} %len_ref.1, bf16[8,768,2,128]{3,2,1,0:T(2,128)(2,1)} %bitcast.161, bf16[8,768,2,128]{3,2,1,0:T(2,128)(2,1)} %bitcast.162, bf16[8,2,128]{2,1,0:T(2,128)(2,1)} %pad_maximum_fusion.5.kn_ref, ...), custom_call_target="tpu_custom_call" | custom-call | flops 1000000000 | bytes 12582912 | tf_op jit(solution)/shard_map/cache_update/pallas_call | solution.py:401
  69.6 3.0 fusion.160
  72.6 2.5 fusion.59
  75.1 4.6 %fusion.19 = f32[8,4096]{1,0:T(8,128)S(1)} fusion(bf16[1,2,1,512,4096]{4,3,2,1,0:T(8,128)(2,1)} %param.28, bf16[8,2,512]{2,1,0:T(2,128)(2,1)S(1)} %reshape.369), kind=kOutput, calls=%fused_computation.19 | convolution fusion | flops 67108864 | bytes 8536064 | tf_op jit(solution)/shard_map/bif,ifd->bd/dot_general | solution.py:427
  79.7 17.7 %all-reduce.2 = bf16[8,4096]{1,0:T(8,128)(2,1)S(1)} all-reduce(f32[8,4096]{1,0:T(8,128)S(1)} %fusion.19), channel_id=1, replica_groups=mesh['pair'=1,'tp'=4,'side'=8] {'tp'}, use_global_device_ids=true, to_apply=%region_8.9 | all-reduce | flops 32768 | bytes 196608 | tf_op jit(solution)/shard_map/psum | solution.py:427
  97.4 0.1 fusion.93
  97.6 28.3 %fusion.16 = bf16[8,2,3584]{2,0,1:T(8,128)(2,1)S(1)} fusion(bf16[4096,2,3584]{2,1,0:T(2,128)(2,1)} %bitcast.155, bf16[8,4096]{1,0:T(8,128)(2,1)S(1)} %get-tuple-element.31, f32[4096]{0:T(1024)S(1)} %bitcast.168, f32[8]{0:T(128)S(1)} %add_rsqrt_fusion.1), kind=kOutput, calls=%fused_computation.18 | convolution fusion | flops 469950464 | bytes 58916896 | tf_op jit(solution)/shard_map/sd,dkf->skf/dot_general | solution.py:37
  125.9 11.4 %fusion.5 = f32[8,4096]{1,0:T(8,128)S(1)} fusion(bf16[1,3584,4096]{2,1,0:T(8,128)(2,1)} %param.30, bf16[8,2,3584]{2,0,1:T(8,128)(2,1)S(1)} %fusion.16), kind=kOutput, calls=%fused_computation.5 | convolution fusion | flops 235110400 | bytes 29605888 | tf_op jit(solution)/shard_map/dot_general | solution.py:430
  137.2 16.3 %all-reduce.3 = bf16[8,4096]{1,0:T(8,128)(2,1)S(1)} all-reduce(f32[8,4096]{1,0:T(8,128)S(1)} %fusion.5), channel_id=1, replica_groups=mesh['pair'=1,'tp'=4,'side'=8] {'tp'}, use_global_device_ids=true, to_apply=%region_10.11 | all-reduce | flops 32768 | bytes 196608 | tf_op jit(solution)/shard_map/psum | solution.py:430
  153.6 1.3 dynamic-slice_bitcast_fusion.1
  154.9 0.8 fusion.70
  155.7 1.1 pad_maximum_fusion.attn
  156.8 1.1 pad_maximum_fusion.1.xown
  157.8 229.2 %prefill_tail.1 = (bf16[512,4096]{1,0:T(8,128)(2,1)}, bf16[28,2,4096,128]{3,2,1,0:T(8,128)(2,1)}) custom-call(bf16[2,256,1024]{2,1,0:T(8,128)(2,1)} %pad_maximum_fusion.attn, bf16[2,64,4096]{2,1,0:T(8,128)(2,1)} %pad_maximum_fusion.1.xown, bf16[1,4096]{1,0:T(2,128)(2,1)} %get-tuple-element.54.gain, bf16[1024,4096]{1,0:T(8,128)(2,1)} %bitcast.174, ...), custom_call_target="tpu_custom_call" | custom-call | flops 45097156608 | bytes 117440512 | tf_op jit(solution)/shard_map/prefill_tail/pallas_call | solution.py:311
  387.1 0.6 fusion.96
  387.7 0.0 collective-permute-done
  387.7 0.0 collective-permute-done.1
  387.7 1.1 select_bitcast_fusion
  388.9 1.0 copy.107
  389.8 1.0 copy.108
  390.8 4.7 %copy.167 = bf16[512,4096]{1,0:T(8,128)(2,1)} copy(bf16[512,4096]{1,0:T(8,128)(2,1)} %get-tuple-element.80) | data formatting | bytes 8388608
  (23 shorter events, 0.3 us)
Async XLA Ops:
  0.7 4.6 %copy-start = (bf16[512,4096]{1,0:T(8,128)(2,1)S(1)}, bf16[512,4096]{1,0:T(8,128)(2,1)}, u32[]{:S(2)}) copy-start(bf16[512,4096]{1,0:T(8,128)(2,1)} %param.16) | copy-start | bytes 12582916
  16.8 12.3 %copy-start.4 = (bf16[1,2,4096]{2,1,0:T(2,128)(2,1)S(1)}, bf16[1,2,4096]{2,1,0:T(2,128)(2,1)}, u32[]{:S(2)}) copy-start(bf16[1,2,4096]{2,1,0:T(2,128)(2,1)} %param.31) | copy-start | bytes 49156
  16.8 12.3 %copy-start.3 = (bf16[8,4096]{1,0:T(8,128)(2,1)S(1)}, bf16[8,4096]{1,0:T(8,128)(2,1)}, u32[]{:S(2)}) copy-start(bf16[8,4096]{1,0:T(8,128)(2,1)} %param.18) | copy-start | bytes 196612
  19.1 18.1 %copy-start.1 = (bf16[512,2,64]{2,0,1:T(8,128)(2,1)}, bf16[512,2,64]{2,0,1:T(8,128)(2,1)S(1)}, u32[]{:S(2)}) copy-start(bf16[512,2,64]{2,0,1:T(8,128)(2,1)S(1)} %get-tuple-element.41) | copy-start | bytes 393220
  20.1 367.7 %collective-permute-start = (bf16[2,512,128]{2,1,0:T(8,128)(2,1)}, bf16[2,512,128]{2,1,0:T(8,128)(2,1)}, u32[]{:S(2)}, u32[]{:S(2)}) collective-permute-start(bf16[2,512,128]{2,1,0:T(8,128)(2,1)} %fusion.83), channel_id=1, source_target_pairs={{0,4},{1,5},{2,6},{3,7},{4,0},{5,1},{6,2},{7,3},{8,20},{9,21},{10,... | collective-permute-start | bytes 786440 | tf_op jit(solution)/shard_map/ppermute | solution.py:380
  21.7 366.1 %collective-permute-start.1 = (bf16[2,512,128]{2,1,0:T(8,128)(2,1)}, bf16[2,512,128]{2,1,0:T(8,128)(2,1)}, u32[]{:S(2)}, u32[]{:S(2)}) collective-permute-start(bf16[2,512,128]{2,1,0:T(8,128)(2,1)} %fusion.77), channel_id=1, source_target_pairs={{0,12},{1,13},{2,14},{3,15},{4,8},{5,9},{6,10},{7,11},{8,28},{9,29... | collective-permute-start | bytes 786440 | tf_op jit(solution)/shard_map/ppermute | solution.py:380
  29.2 8.1 %copy-start.5 = (s32[8]{0:T(128)S(1)}, s32[8]{0:T(128)}, u32[]{:S(2)}) copy-start(s32[8]{0:T(128)} %len_ref.1) | copy-start | bytes 100
  50.9 3.1 copy-start.2
  57.5 2.1 copy-start.6
